TPU v7x, 32 devices: a 4x2x2 block of a 4x4x8 slice. The times are simulated.
32 devices in a mesh: dp: 4 (over y, z), sp: 8 (over x, core).
Axes of the slice: x: 4, y: 2, z: 2, core: 2. Of those that a mesh axis runs over, the one named last changes fastest.
The devices are a block of a 4x4x8 slice.
Arguments:
- hidden_in: bfloat16 [32768, 1152], P(('dp', 'sp')), parts along dimension 0
- w_query: bfloat16 [1152, 4, 256], replicated
- w_key: bfloat16 [1152, 1, 256], replicated
- w_value: bfloat16 [1152, 1, 256], replicated
- w_out: bfloat16 [4, 256, 1152], replicated
- w_up: bfloat16 [1152, 6912], replicated
- w_down: bfloat16 [6912, 1152], replicated
- rel_bias: float32 [4, 1025], replicated
- glob_pos: int32 [1024], P('dp'), parts along dimension 0
Outputs:
- output 1: bfloat16 [32768, 1152], P(('dp', 'sp')), parts along dimension 0
- output 2: bfloat16 [1024, 1152], P('dp'), parts along dimension 0
There are 4 independent parts. A program takes and returns all parts, laid end to end along the dimension named above; an argument that names none is the same for every part.
All inputs are finite; a program needn't handle non-finite values.
Results may differ from a plain program's by a relative error of at most 0.00839907.
Values are sent between devices in bfloat16 or wider.
A program may use at most 768 MiB of HBM per device.

v0:
```python
import jax
import jax.numpy as jnp
from jax import lax
from jax.sharding import PartitionSpec as P


def three_blocks(ext, width):
    blocks = ext.reshape((ext.shape[0] // width, width) + ext.shape[1:])
    return jnp.concatenate([blocks[:-2], blocks[1:-1], blocks[2:]], axis=1)


def bias_tile(rel_bias, kv_heads):
    heads, span = rel_bias.shape
    width = (span - 1) // 2
    padded = jnp.pad(rel_bias, ((0, 0), (0, width)))
    tiled = jnp.tile(padded, (1, width))[:, : 3 * width * width]
    return tiled.reshape(kv_heads, heads // kv_heads, width, 3 * width)


def project(hidden_in, w_query, w_key, w_value):
    head = w_query.shape[2]
    queries = (jnp.einsum('td,dhe->the', hidden_in, w_query, preferred_element_type=jnp.float32) * head ** -0.5).astype(jnp.bfloat16)
    keys_loc = jnp.einsum('td,dge->tge', hidden_in, w_key, preferred_element_type=jnp.float32).astype(jnp.bfloat16)
    vals_loc = jnp.einsum('td,dge->tge', hidden_in, w_value, preferred_element_type=jnp.float32).astype(jnp.bfloat16)
    return queries, keys_loc, vals_loc


def window_attention(query_blk, key_win, val_win, key_ok, bias, key_glob, val_glob):
    width = query_blk.shape[1]
    row_idx = jnp.arange(width)[:, None]
    col_idx = jnp.arange(3 * width)[None, :]
    band = jnp.abs(col_idx - width - row_idx) <= width
    mask = band & key_ok[:, None, None, None, :]
    score_win = jnp.einsum('bqgrd,bkgd->bgrqk', query_blk, key_win, preferred_element_type=jnp.float32) + bias
    score_win = jnp.where(mask, score_win, -1e30)
    score_glob = jnp.einsum('bqgrd,ngd->bgrqn', query_blk, key_glob, preferred_element_type=jnp.float32)
    top = jnp.maximum(score_win.max(-1), score_glob.max(-1))[..., None]
    prob_win = jnp.exp(score_win - top)
    prob_glob = jnp.exp(score_glob - top)
    norm_sum = prob_win.sum(-1) + prob_glob.sum(-1)
    weighted = jnp.einsum('bgrqk,bkgd->bqgrd', prob_win.astype(jnp.bfloat16), val_win, preferred_element_type=jnp.float32)
    weighted = weighted + jnp.einsum('bgrqn,ngd->bqgrd', prob_glob.astype(jnp.bfloat16), val_glob, preferred_element_type=jnp.float32)
    return weighted / jnp.moveaxis(norm_sum, 3, 1)[..., None]


def global_partial(query_glob, keys_loc, vals_loc):
    scores = jnp.einsum('ngrd,tgd->ngrt', query_glob, keys_loc, preferred_element_type=jnp.float32)
    top = scores.max(-1)
    weights = jnp.exp(scores - top[..., None])
    weighted = jnp.einsum('ngrt,tgd->ngrd', weights.astype(jnp.bfloat16), vals_loc, preferred_element_type=jnp.float32)
    return top, weights.sum(-1), weighted


def finish_layer(hidden_in, attended, w_out, w_up, w_down):
    hidden = (hidden_in.astype(jnp.float32) + jnp.einsum('the,hed->td', attended, w_out, preferred_element_type=jnp.float32)).astype(jnp.bfloat16)
    upper = jax.nn.gelu(jnp.dot(hidden, w_up, preferred_element_type=jnp.float32)).astype(jnp.bfloat16)
    return (hidden.astype(jnp.float32) + jnp.dot(upper, w_down, preferred_element_type=jnp.float32)).astype(jnp.bfloat16)


def solution(mesh):
    sp_size = mesh.shape['sp']
    to_right = [(src, src + 1) for src in range(sp_size - 1)]
    to_left = [(src + 1, src) for src in range(sp_size - 1)]

    def shard_layer(hidden_in, w_query, w_key, w_value, w_out, w_up, w_down, rel_bias, glob_pos):
        rows = hidden_in.shape[0]
        heads, head = w_query.shape[1], w_query.shape[2]
        kv_heads = w_key.shape[1]
        group = heads // kv_heads
        width = (rel_bias.shape[1] - 1) // 2
        n_glob = glob_pos.shape[0]
        seq_len = rows * sp_size
        start = lax.axis_index('sp') * rows
        queries, keys_loc, vals_loc = project(hidden_in, w_query, w_key, w_value)
        owner = glob_pos[:, None] == (start + jnp.arange(rows))[None, :]
        pick = owner.astype(jnp.bfloat16)
        query_pick = jnp.einsum('nt,the->nhe', pick, queries, preferred_element_type=jnp.float32).astype(jnp.bfloat16)
        key_pick = jnp.einsum('nt,tge->nge', pick, keys_loc, preferred_element_type=jnp.float32).astype(jnp.bfloat16)
        val_pick = jnp.einsum('nt,tge->nge', pick, vals_loc, preferred_element_type=jnp.float32).astype(jnp.bfloat16)
        query_glob, key_glob, val_glob = lax.psum((query_pick, key_pick, val_pick), 'sp')
        keyval_loc = jnp.concatenate([keys_loc, vals_loc], axis=1)
        from_left = lax.ppermute(keyval_loc[rows - width:], 'sp', to_right)
        from_right = lax.ppermute(keyval_loc[:width], 'sp', to_left)
        keyval_ext = jnp.concatenate([from_left, keyval_loc, from_right], axis=0)
        ext_pos = start - width + jnp.arange(rows + 2 * width)
        is_glob_key = jnp.any(glob_pos[:, None] == ext_pos[None, :], axis=0)
        key_ok = (ext_pos >= 0) & (ext_pos < seq_len) & jnp.logical_not(is_glob_key)
        out_win = window_attention(
            queries.reshape(rows // width, width, kv_heads, group, head),
            three_blocks(keyval_ext[:, :kv_heads], width), three_blocks(keyval_ext[:, kv_heads:], width),
            three_blocks(key_ok, width), bias_tile(rel_bias, kv_heads), key_glob, val_glob)
        top, total, weighted = global_partial(query_glob.reshape(n_glob, kv_heads, group, head), keys_loc, vals_loc)
        best = lax.pmax(top, 'sp')
        rescale = jnp.exp(top - best)
        total, weighted = lax.psum((total * rescale, weighted * rescale[..., None]), 'sp')
        out_glob = (weighted / total[..., None]).astype(jnp.bfloat16).reshape(n_glob, heads, head)
        placed = jnp.einsum('nt,nhe->the', pick, out_glob, preferred_element_type=jnp.float32)
        is_glob_row = jnp.any(owner, axis=0)
        attended = jnp.where(is_glob_row[:, None, None], placed, out_win.reshape(rows, heads, head)).astype(jnp.bfloat16)
        y_out = finish_layer(hidden_in, attended, w_out, w_up, w_down)
        y_pick = jnp.einsum('nt,td->nd', pick, y_out, preferred_element_type=jnp.float32).astype(jnp.bfloat16)
        return y_out, lax.psum(y_pick, 'sp')

    return jax.shard_map(
        shard_layer, mesh=mesh,
        in_specs=(P(('dp', 'sp'), None), P(), P(), P(), P(), P(), P(), P(), P('dp')),
        out_specs=(P(('dp', 'sp'), None), P('dp', None)),
        check_vma=False)
```

profile of v0, /device:TPU:81, one launch (start us, length us, event | category | flops | bytes accessed | tf_op | source)
XLA Modules:
  0.0 336.0 jit_solution(2782658160366692767)
XLA Ops:
  7.2 0.1 all-reduce.10.cloned.1.call-start
  7.3 2.8 convolution_convert_fusion.1
  10.1 0.8 convolution_convert_fusion.2
  10.9 1.1 fusion.86
  12.0 4.6 %collective-permute-start = (bf16[512,2,256]{2,0,1:T(8,128)(2,1)}, bf16[512,2,256]{2,0,1:T(8,128)(2,1)}, u32[]{:S(2)}, u32[]{:S(2)}) collective-permute-start(bf16[512,2,256]{2,0,1:T(8,128)(2,1)} %get-tuple-element.11), channel_id=1, source_target_pairs={{0,1},{1,2},{2,3},{3,4},{4,5},{5,6},{6,7},{8,9},{9,10},{10,11},{11... | collective-permute-start | bytes 1572872 | tf_op jit(solution)/shard_map/ppermute | solution.py:82
  16.6 2.0 collective-permute-start.1
  18.6 1.0 fusion.75
  19.6 1.0 fusion.78
  20.6 5.2 %multiply_convert_fusion = bf16[1024,4,256]{2,0,1:T(8,128)(2,1)S(1)} fusion(bf16[1152,4,256]{2,1,0:T(4,128)(2,1)} %param.10, bf16[1024,1152]{1,0:T(8,128)(2,1)} %param.9), kind=kOutput, calls=%fused_computation.32 | convolution fusion | flops 2418016256 | bytes 6815744 | tf_op jit(solution)/shard_map/td,dhe->the/dot_general | solution.py:22
  25.9 1.3 copy-done.4
  27.2 1.6 convolution_convert_fusion.3
  28.8 0.6 all-reduce.6.cloned.1.call-start
  29.4 0.8 compare_reduce_fusion
  30.2 5.8 %tile.4 = f32[4,512,1537]{2,1,0:T(8,128)} broadcast(f32[4,1537]{1,0:T(4,128)S(1)} %pad.4), dimensions={0,2} | broadcast | bytes 12615696 | tf_op jit(solution)/shard_map/tile | solution.py:16
  36.0 20.2 %reshape.216 = f32[3147776]{0:T(1024)} reshape(f32[4,512,1537]{2,1,0:T(8,128)} %tile.4) | data formatting | bytes 25182208
  56.1 15.0 %tile.10 = f32[4,786944]{1,0:T(4,128)} reshape(f32[3147776]{0:T(1024)} %reshape.216) | data formatting | bytes 25182208 | tf_op jit(solution)/shard_map/tile | solution.py:16
  71.1 10.5 %slice.91 = f32[4,786432]{1,0:T(4,128)} slice(f32[4,786944]{1,0:T(4,128)} %tile.10), slice={[0:4], [0:786432]} | slice | bytes 25165824 | tf_op jit(solution)/shard_map/slice | solution.py:16
  81.7 13.2 %copy.75 = f32[1,4,512,1536]{3,2,1,0:T(8,128)} copy(f32[1,4,512,1536]{3,1,2,0:T(4,128)} %bitcast.203) | data formatting | bytes 25165824
  94.9 12.7 %copy.42 = f32[4,512,1536]{1,2,0:T(8,128)} copy(f32[4,512,1536]{2,1,0:T(8,128)} %bitcast.204) | data formatting | bytes 25165824 | tf_op jit(solution)/shard_map/add | solution.py:34
  107.6 0.4 compare_reduce_fusion.1
  108.0 1.8 abs_compare_fusion
  109.8 1.0 copy.39
  110.8 2.8 broadcast_and_fusion
  113.6 1.8 bitcast_reduce_fusion.1
  115.4 1.9 copy-done.2
  117.3 0.6 fusion.28
  117.9 12.8 %pmax.7 = f32[256,1,4]{0,2,1:T(4,128)S(1)} all-reduce(f32[256,1,4]{0,2,1:T(4,128)S(1)} %bitcast.218), channel_id=1, replica_groups=mesh['dp'=4,'sp'=8] {'sp'}, use_global_device_ids=true, to_apply=%region_3.0 | all-reduce | flops 1024 | bytes 8192 | tf_op jit(solution)/shard_map/pmax | solution.py:93
  130.7 3.9 %fusion.72 = f32[256,1,4,256]{0,3,2,1:T(8,128)} fusion(f32[1024,256,4]{1,0,2:T(8,128)} %copy-done.2, f32[256,4]{0,1:T(4,128)S(1)} %get-tuple-element.22, bf16[1024,256]{1,0:T(8,128)(2,1)S(1)} %convolution_convert_fusion.2, f32[256,4]{0,1:T(4,128)S(1)} %get-tuple-element.14), kind=kOutput, calls=%fused_computation.74 | convolution fusion | flops 539230208 | bytes 5775360 | tf_op jit(solution)/shard_map/ngrt,tgd->ngrd/dot_general | solution.py:50
  134.6 0.1 all-reduce.8.cloned.1.call-start
  134.7 15.3 %psum.44 = f32[256,4]{0,1:T(4,128)} all-reduce(f32[256,4]{0,1:T(4,128)S(1)} %get-tuple-element.13), channel_id=1, replica_groups=mesh['dp'=4,'sp'=8] {'sp'}, use_global_device_ids=true, to_apply=%region_6.7 | all-reduce | flops 1024 | bytes 8192 | tf_op jit(solution)/shard_map/psum | solution.py:95
  150.0 4.3 %bitcast_reduce_fusion = (f32[2,4,512]{2,1,0:T(4,128)S(1)}, f32[256,2,512,4]{2,0,3,1:T(8,128)}) fusion(bf16[2,512,4,256]{3,1,0,2:T(8,128)(2,1)} %bitcast.205, bf16[256,256]{1,0:T(8,128)(2,1)S(1)} %copy-done.8), kind=kOutput, calls=%fused_computation.26 | convolution fusion | flops 537915392 | bytes 6438912 | tf_op jit(solution)/shard_map/bqgrd,ngd->bgrqn/dot_general | solution.py:36
  154.3 2.5 pad_maximum_fusion.6
  156.8 15.0 %fusion.11 = (f32[2,4,512]{2,1,0:T(4,128)S(1)}, f32[2,1536,512,4]{2,1,3,0:T(8,128)}) fusion(f32[4,512,1536]{1,2,0:T(8,128)} %copy.42, pred[2,512,1536]{1,2,0:T(8,128)(4,1)} %broadcast_and_fusion, bf16[2,512,4,256]{3,1,0,2:T(8,128)(2,1)} %bitcast.206, bf16[2,512,1,256]{3,1,0,2:T(8,128)(2,1)} %bitcast.214, bf16[2,512,1,256]{3,1,0,2:T(8,128)(2,1)S(1)} %bitcast.209, ...), kind=kOutput, calls=%fused_computation.14 | convolution fusion | flops 3244814336 | bytes 43008000 | tf_op jit(solution)/shard_map/bqgrd,bkgd->bgrqk/dot_general | solution.py:34
  171.8 3.0 fusion.30
  174.8 0.5 copy-done.1
  175.3 2.7 fusion.43
  178.0 13.9 %fusion.9 = f32[2,4,512]{2,1,0:T(4,128)S(1)} fusion(f32[2,1536,512,4]{2,1,3,0:T(8,128)} %get-tuple-element.19, f32[2,4,512]{2,1,0:T(4,128)S(1)} %max.11, f32[4,512,1536]{1,2,0:T(8,128)} %copy.42, pred[2,512,1536]{1,2,0:T(8,128)(4,1)S(1)} %copy-done.3), kind=kLoop, calls=%fused_computation.12 | loop fusion | flops 25161728 | bytes 39354368 | tf_op jit(solution)/shard_map/reduce_sum | solution.py:40
  191.9 1.0 copy.40
  192.9 0.2 copy.38
  193.1 17.2 %fusion.22 = bf16[2,512,1,4,256]{1,4,3,0,2:T(8,128)(2,1)} fusion(f32[256,2,4,512]{3,0,2,1:T(8,128)} %fusion.43, f32[2,1536,512,4]{2,1,3,0:T(8,128)} %get-tuple-element.19, f32[2,4,512]{2,1,0:T(4,128)S(1)} %max.11, f32[4,512,1536]{1,2,0:T(8,128)} %copy.42, pred[2,512,1536]{1,2,0:T(8,128)(4,1)} %broadcast_and_fusion, f32[2,512,4]{1,2,0:T(4,128)S(1)} %add_bitcast_fusion, ...), kind=kOutput, calls=%fused_computation.24 | convolution fusion | flops 3254255616 | bytes 47218688 | tf_op jit(solution)/shard_map/bgrqk,bkgd->bqgrd/dot_general | solution.py:41
  210.3 4.1 %copy.47 = bf16[2,512,1,4,256]{4,1,0,3,2:T(8,128)(2,1)} copy(bf16[2,512,1,4,256]{1,4,3,0,2:T(8,128)(2,1)} %fusion.22) | data formatting | bytes 4194304 | tf_op jit(solution)/shard_map/div | solution.py:43
  214.5 7.8 %fusion.21 = bf16[1024,1152]{1,0:T(8,128)(2,1)} fusion(bf16[1024,1152]{1,0:T(8,128)(2,1)} %param.9, bf16[4,256,1152]{2,1,0:T(8,128)(2,1)S(1)} %copy-done, bf16[1024,4,256]{2,0,1:T(8,128)(2,1)} %bitcast.215, pred[1024]{0:T(1024)(128)(4,1)S(1)} %copy-done.15, f32[256,1,4,256]{0,3,2,1:T(8,128)} %all-reduce.6.cloned.1.call-done, f32[256,4]{0,1:T(4,128)S(1)} %copy-done.12, ...), kind=kOutput, calls=%fused_computation.22 | convolution fusion | flops 2958426112 | bytes 10233856 | tf_op jit(solution)/shard_map/the,hed->td/dot_general | solution.py:55
  222.3 26.8 %fusion.149 = bf16[1024,6912]{1,0:T(8,128)(2,1)S(1)} fusion(bf16[1152,6912]{1,0:T(8,128)(2,1)} %param.14, bf16[1024,1152]{1,0:T(8,128)(2,1)} %fusion.21), kind=kOutput, calls=%fused_computation.8.clone.clone.clone.clone.clone.clone.1 | convolution fusion | flops 16371154944 | bytes 32440320 | tf_op jit(solution)/shard_map/dot_general | solution.py:56
  249.2 21.2 %fusion.25 = bf16[1024,1152]{1,0:T(8,128)(2,1)S(1)} fusion(bf16[6912,1152]{1,0:T(8,128)(2,1)} %param.15, bf16[1024,1152]{1,0:T(8,128)(2,1)S(1)} %copy-done.19, bf16[1024,6912]{1,0:T(8,128)(2,1)S(1)} %fusion.149), kind=kOutput, calls=%fused_computation.33 | convolution fusion | flops 16310992896 | bytes 34799616 | tf_op jit(solution)/shard_map/dot_general | solution.py:57
  270.4 1.4 copy-done.18
  271.8 1.7 convolution_convert_fusion
  273.6 53.7 %all-reduce.8.cloned.1.call-done = bf16[256,1152]{1,0:T(8,128)(2,1)} async-done(((bf16[256,1152]{1,0:T(8,128)(2,1)}), bf16[256,1152]{1,0:T(8,128)(2,1)}) %all-reduce.8.cloned.1.call-update) | async-done | bytes 589840 | tf_op jit(solution)/shard_map/psum | solution.py:102
  327.3 1.9 copy.81
  (55 shorter events, 0.4 us)
Async XLA Ops:
  7.2 207.3 %copy-start = (bf16[4,256,1152]{2,1,0:T(8,128)(2,1)S(1)}, bf16[4,256,1152]{2,1,0:T(8,128)(2,1)}, u32[]{:S(2)}) copy-start(bf16[4,256,1152]{2,1,0:T(8,128)(2,1)} %param.13) | copy-start | bytes 7077892
  7.2 106.4 %all-reduce.10.cloned.1.call-start = ((), (), s32[]{:S(2)}) async-start(), calls=%async_computation.2 | async-start | bytes 1572864 | tf_op jit(solution)/shard_map/psum | solution.py:80
  7.3 2.8 copy-start.16
  7.3 2.8 copy-start.17
  10.1 8.5 %copy-start.13 = (s32[256]{0:T(256)S(1)}, s32[256]{0:T(256)}, u32[]{:S(2)}) copy-start(s32[256]{0:T(256)} %param.17) | copy-start | bytes 3076
  12.0 142.3 %collective-permute-start = (bf16[512,2,256]{2,0,1:T(8,128)(2,1)}, bf16[512,2,256]{2,0,1:T(8,128)(2,1)}, u32[]{:S(2)}, u32[]{:S(2)}) collective-permute-start(bf16[512,2,256]{2,0,1:T(8,128)(2,1)} %get-tuple-element.11), channel_id=1, source_target_pairs={{0,1},{1,2},{2,3},{3,4},{4,5},{5,6},{6,7},{8,9},{9,10},{10,11},{11... | collective-permute-start | bytes 1572872 | tf_op jit(solution)/shard_map/ppermute | solution.py:82
  16.6 137.7 %collective-permute-start.1 = (bf16[512,2,256]{2,0,1:T(8,128)(2,1)}, bf16[512,2,256]{2,0,1:T(8,128)(2,1)}, u32[]{:S(2)}, u32[]{:S(2)}) collective-permute-start(bf16[512,2,256]{2,0,1:T(8,128)(2,1)} %get-tuple-element.12), channel_id=1, source_target_pairs={{1,0},{2,1},{3,2},{4,3},{5,4},{6,5},{7,6},{9,8},{10,9},{11,10},{12... | collective-permute-start | bytes 1572872 | tf_op jit(solution)/shard_map/ppermute | solution.py:83
  18.6 10.8 %copy-start.10 = (s32[1024]{0:T(1024)}, s32[1024]{0:T(1024)S(1)}, u32[]{:S(2)}) copy-start(s32[1024]{0:T(1024)S(1)} %iota_add_fusion.2) | copy-start | bytes 12292
  25.9 1.3 copy-start.4
  27.2 3.0 copy-start.9
  28.8 185.6 %all-reduce.6.cloned.1.call-start = ((), (), s32[]{:S(2)}) async-start(), calls=%async_computation | async-start | bytes 2097152 | tf_op jit(solution)/shard_map/psum | solution.py:95
  115.4 1.9 copy-start.2
  117.9 32.1 %copy-start.8 = (bf16[256,256]{1,0:T(8,128)(2,1)S(1)}, bf16[256,256]{1,0:T(8,128)(2,1)}, u32[]{:S(2)}) copy-start(bf16[256,256]{1,0:T(8,128)(2,1)} %get-tuple-element.2) | copy-start | bytes 393220
  134.6 192.6 %all-reduce.8.cloned.1.call-start = ((), (), s32[]{:S(2)}) async-start(), calls=%async_computation.1 | async-start | bytes 1179648 | tf_op jit(solution)/shard_map/psum | solution.py:102
  156.8 18.0 %copy-start.7 = (bf16[256,256]{1,0:T(8,128)(2,1)S(1)}, bf16[256,256]{1,0:T(8,128)(2,1)}, u32[]{:S(2)}) copy-start(bf16[256,256]{1,0:T(8,128)(2,1)} %get-tuple-element.3) | copy-start | bytes 393220
  171.8 3.4 %copy-start.1 = (f32[256,2,512,4]{2,0,3,1:T(8,128)S(1)}, f32[256,2,512,4]{2,0,3,1:T(8,128)}, u32[]{:S(2)}) copy-start(f32[256,2,512,4]{2,0,3,1:T(8,128)} %get-tuple-element.21) | copy-start | bytes 12582916
  175.3 2.7 copy-start.3
  178.0 13.9 %copy-start.6 = (bf16[1024,1,256]{2,0,1:T(8,128)(2,1)S(1)}, bf16[1024,1,256]{2,0,1:T(8,128)(2,1)}, u32[]{:S(2)}) copy-start(bf16[1024,1,256]{2,0,1:T(8,128)(2,1)} %get-tuple-element.10) | copy-start | bytes 1572868
  178.0 14.9 %copy-start.5 = (bf16[1024,1,256]{2,0,1:T(8,128)(2,1)S(1)}, bf16[1024,1,256]{2,0,1:T(8,128)(2,1)}, u32[]{:S(2)}) copy-start(bf16[1024,1,256]{2,0,1:T(8,128)(2,1)} %get-tuple-element.5) | copy-start | bytes 1572868
  210.3 4.2 %copy-start.11 = (s32[1024]{0:T(1024)S(1)}, s32[1024]{0:T(1024)}, u32[]{:S(2)}) copy-start(s32[1024]{0:T(1024)} %copy-done.10) | copy-start | bytes 12292
  210.3 4.2 %copy-start.12 = (f32[256,4]{0,1:T(4,128)S(1)}, f32[256,4]{0,1:T(4,128)}, u32[]{:S(2)}) copy-start(f32[256,4]{0,1:T(4,128)} %psum.44) | copy-start | bytes 12292
  210.3 4.2 %copy-start.14 = (s32[256]{0:T(256)S(1)}, s32[256]{0:T(256)}, u32[]{:S(2)}) copy-start(s32[256]{0:T(256)} %param.17) | copy-start | bytes 3076
  210.3 4.2 %copy-start.15 = (pred[1024]{0:T(1024)(128)(4,1)S(1)}, pred[1024]{0:T(1024)(128)(4,1)}, u32[]{:S(2)}) copy-start(pred[1024]{0:T(1024)(128)(4,1)} %compare_reduce_fusion) | copy-start | bytes 3076
  222.3 26.8 %copy-start.19 = (bf16[1024,1152]{1,0:T(8,128)(2,1)S(1)}, bf16[1024,1152]{1,0:T(8,128)(2,1)}, u32[]{:S(2)}) copy-start(bf16[1024,1152]{1,0:T(8,128)(2,1)} %fusion.21) | copy-start | bytes 7077892
  270.4 1.4 copy-start.18
Sparse Core Ops, SparseCore 0:
  28.9 56.8 all-reduce.9
  134.7 56.7 all-reduce.5
  273.7 53.5 all-reduce.7
where the time goes:
time: 341 us; the launch traced here: 336 us
  matrix products  115 us (34%)
  local copies, waits for them, and re-layouts  90.8 us (27%)
  waiting for transfers between devices  53.8 us (16%)
  blocking collectives  28 us (8%)
  other arithmetic  26.8 us (8%)
  between operations  14.4 us (4%)
  starting transfers between devices  7.26 us (2%)
    psum x1, waiting for transfers between devices, shard_layer(): return (y_out, lax.psum(y_pick, 'sp'))  53.7 us
    unnamed x43, local copies, waits for them, and re-layouts  40.4 us
    dot_general x1, matrix products, finish_layer(): jnp.dot(hidden, w_up, preferred_element_type=jnp.float32)  26.8 us
    dot_general x1, matrix products, finish_layer(): jnp.dot(upper, w_down, preferred_element_type=jnp.float32)  21.2 us
    another operation x2, local copies, waits for them, and re-layouts, bias_tile(): tiled = jnp.tile(padded, (1, width))[:, :3 * width * width]  20.8 us
    dot_general x1, matrix products, window_attention(): jnp.einsum('bgrqk,bkgd->bqgrd', prob_win.astype(jnp.bfloat16), val_win, p...  17.2 us
    reduce_sum x2, other arithmetic, window_attention(): norm_sum = prob_win.sum(-1) + prob_glob.sum(-1)  16.8 us
    psum x1, blocking collectives, shard_layer(): lax.psum((total * rescale, weighted * rescale[..., None]), 'sp')  15.3 us
  transfers between devices with their start and end apart: 5, of which 1 were waited for; matrix products, arithmetic and copies ran while one was open for 49% of the time, Pallas kernels for 0%

commit v1 on v0

v1 whole, which is shorter than its diff:
```python
import functools

import jax
import jax.numpy as jnp
from jax import lax
from jax.experimental import pallas as pl
from jax.experimental.pallas import tpu as pltpu
from jax.sharding import PartitionSpec as P

MESH = pl.DeviceIdType.MESH
F32 = jnp.float32
BF16 = jnp.bfloat16
QB = 128
VMEM_LIMIT = 60 * 1024 * 1024


def mm(a, b):
    return jnp.dot(a, b, preferred_element_type=F32)


def mm_ta(a, b):
    return lax.dot_general(a, b, (((0,), (0,)), ((), ())), preferred_element_type=F32)


def mm_tb(a, b):
    return lax.dot_general(a, b, (((1,), (1,)), ((), ())), preferred_element_type=F32)


def send(src, dst, ssem, rsem, dev):
    copy = pltpu.make_async_remote_copy(
        src_ref=src, dst_ref=dst, send_sem=ssem, recv_sem=rsem, device_id={'sp': dev}, device_id_type=MESH)
    copy.start()
    return copy


def arrival(ref, ssem, rsem, dev):
    return pltpu.make_async_remote_copy(
        src_ref=ref, dst_ref=ref, send_sem=ssem, recv_sem=rsem, device_id={'sp': dev}, device_id_type=MESH)


def greet(sp):
    me = lax.axis_index('sp')
    barrier = pltpu.get_barrier_semaphore()
    for k in range(1, sp):
        pl.semaphore_signal(barrier, inc=1, device_id={'sp': lax.rem(me + k, sp)}, device_id_type=MESH)
    return barrier


def gather_blocks(buf, chips, chip, core, ssem, rsem):
    sends = []
    mine = buf.at[core * chips + chip]
    for k in range(1, chips):
        peer = lax.rem(chip + k, chips) * 2 + core
        sends.append(send(mine, mine, ssem.at[k], rsem.at[k], peer))
    return sends


def gather_forward(buf, chips, chip, core, ssem, rsem):
    partner = chip * 2 + 1 - core
    for k in range(1, chips):
        src = lax.rem(chip - k + chips, chips)
        arrival(buf.at[core * chips + src], ssem.at[k], rsem.at[k], partner).wait_recv()
    half = buf.at[pl.ds(core * chips, chips)]
    return send(half, half, ssem.at[0], rsem.at[0], partner)


def gather_finish(buf, chips, chip, core, ssem, rsem, sends):
    partner = chip * 2 + 1 - core
    other = buf.at[pl.ds((1 - core) * chips, chips)]
    arrival(other, ssem.at[0], rsem.at[0], partner).wait_recv()
    for copy in sends:
        copy.wait_send()


def attention_kernel(sp, heads, x_hbm, wq_hbm, wk_hbm, wv_hbm, wo_hbm, rel_ref, gp_ref, h_ref,
                     x_ref, wq_ref, wk_ref, wv_ref, wo_ref, rel_pad, tile, onehot, kmask,
                     kt, kloc, vt, vext, qs, qg, ktg, vg, att,
                     xp, xq, xs, xr, xg, part, pq, pc, pr,
                     load_sem, halo_s, halo_r, pick_s, pick_r, xg_s, xg_r, part_s, part_r):
    me = lax.axis_index('sp')
    chips = sp // 2
    chip, core = me // 2, lax.rem(me, 2)
    partner = chip * 2 + 1 - core
    rows, dim = x_ref.shape
    head = wk_ref.shape[1]
    width = (rel_ref.shape[1] - 1) // 2
    span = 2 * width + QB
    n_glob = gp_ref.shape[1]
    share = n_glob // sp
    ext = rows + 2 * width
    seq = rows * sp
    start = me * rows
    ninf = -jnp.inf

    loads = []
    for i, (src, dst) in enumerate(((x_hbm, x_ref), (wk_hbm, wk_ref), (wv_hbm, wv_ref), (wq_hbm, wq_ref), (wo_hbm, wo_ref))):
        copy = pltpu.make_async_copy(src, dst, load_sem.at[i])
        copy.start()
        loads.append(copy)
    barrier = greet(sp)

    pos = start - width + lax.broadcasted_iota(jnp.int32, (ext, n_glob), 0)
    onehot[...] = jnp.where(pos == gp_ref[...], 1.0, 0.0).astype(BF16)
    count = mm_tb(jnp.ones((8, n_glob), BF16), onehot[...])[0:1]
    col = start - width + lax.broadcasted_iota(jnp.int32, (1, ext), 1)
    kmask[...] = jnp.where((count > 0.5) | (col < 0) | (col >= seq), ninf, 0.0)
    rel_pad[...] = jnp.full(rel_pad.shape, ninf, F32)
    rel_pad[:, : 2 * width + 1] = rel_ref[...]
    for h in range(heads):
        line = jnp.broadcast_to(rel_pad[h : h + 1, :], (QB, span))
        tile[h * QB : (h + 1) * QB, :] = pltpu.roll(line, 0, 1, stride=1, stride_axis=0)

    loads[0].wait()
    own = onehot[width : width + rows, :]
    picked = mm_ta(own, x_ref[...]).astype(BF16)
    xp[...] = picked.reshape(xp.shape)
    pl.semaphore_wait(barrier, sp - 1)
    pick_send = [send(xp.at[1 - core], xq, pick_s.at[0], pick_r.at[0], partner)]

    loads[1].wait()
    loads[2].wait()
    k32 = mm(x_ref[...], wk_ref[...])
    kloc[...] = k32.astype(BF16)
    kt[:, width : width + rows] = k32.T.astype(BF16)
    v32 = mm(x_ref[...], wv_ref[...])
    vext[width : width + rows, :] = v32.astype(BF16)
    vt[...] = v32.T.astype(BF16)
    right, left = lax.rem(me + 1, sp), lax.rem(me + sp - 1, sp)
    halo = [
        send(kt.at[:, pl.ds(rows, width)], kt.at[:, pl.ds(0, width)], halo_s.at[0], halo_r.at[0], right),
        send(vext.at[pl.ds(rows, width)], vext.at[pl.ds(0, width)], halo_s.at[1], halo_r.at[1], right),
        send(kt.at[:, pl.ds(width, width)], kt.at[:, pl.ds(width + rows, width)], halo_s.at[2], halo_r.at[2], left),
        send(vext.at[pl.ds(width, width)], vext.at[pl.ds(width + rows, width)], halo_s.at[3], halo_r.at[3], left),
    ]

    arrival(xq, pick_s.at[0], pick_r.at[0], partner).wait_recv()
    xs[...] = xp[core] + xq[...]
    for k in range(1, chips):
        there = lax.rem(chip + k, chips)
        pick_send.append(send(xs.at[there], xr.at[k - 1], pick_s.at[k], pick_r.at[k], there * 2 + core))

    loads[3].wait()
    scale = head ** -0.5

    def project(b, carry):
        xb = x_ref[pl.ds(b * 2 * QB, 2 * QB), :]
        qb = (mm(xb, wq_ref[...]) * scale).astype(BF16)
        for r in range(2):
            for h in range(heads):
                qs[2 * b + r, h * QB : (h + 1) * QB, :] = qb[r * QB : (r + 1) * QB, h * head : (h + 1) * head]
        return carry

    lax.fori_loop(0, rows // (2 * QB), project, 0)

    for k in range(1, chips):
        arrival(xr.at[k - 1], pick_s.at[k], pick_r.at[k], partner).wait_recv()
    mine = xs[chip]
    for k in range(1, chips):
        mine = mine + xr[k - 1]
    xg[core * chips + chip] = mine
    xg_send = gather_blocks(xg, chips, chip, core, xg_s, xg_r)
    for copy in pick_send:
        copy.wait_send()
    xg_send.append(gather_forward(xg, chips, chip, core, xg_s, xg_r))
    gather_finish(xg, chips, chip, core, xg_s, xg_r, xg_send)

    xgv = xg[...].reshape(n_glob, dim)
    qgv = (mm(xgv, wq_ref[...]) * scale).astype(BF16)
    ktg[...] = mm(xgv, wk_ref[...]).T.astype(BF16)
    vg[...] = mm(xgv, wv_ref[...]).astype(BF16)
    for r in range(sp):
        for h in range(heads):
            qg[r, h * share : (h + 1) * share, :] = qgv[r * share : (r + 1) * share, h * head : (h + 1) * head]

    cols = heads * share

    def partial(c, carry):
        s = mm_tb(kloc[...], qg[pl.ds(2 * c, 2)].reshape(2 * cols, head))
        top = jnp.max(s, axis=0, keepdims=True)
        e = jnp.exp(s - top)
        total = jnp.sum(e, axis=0, keepdims=True)
        num = mm(vt[...], e.astype(BF16))
        stats = jnp.concatenate([top, total, jnp.zeros((6, 2 * cols), F32)], axis=0)
        for r in range(2):
            part[c // (chips // 2), lax.rem(c, chips // 2) * 2 + r, 0:head, :] = num[:, r * cols : (r + 1) * cols]
            part[c // (chips // 2), lax.rem(c, chips // 2) * 2 + r, head:, :] = stats[:, r * cols : (r + 1) * cols]
        return carry

    lax.fori_loop(0, sp // 2, partial, 0)
    part_send = [send(part.at[1 - core], pq, part_s.at[0], part_r.at[0], partner)]

    def merge(blocks):
        best = functools.reduce(jnp.maximum, [b[1] for b in blocks])
        num, total = 0.0, 0.0
        for n, t, l in blocks:
            f = jnp.exp(t - best)
            num = num + n * f
            total = total + l * f
        return num, best, total

    def read(ref, i):
        return ref[i, 0:head, :], ref[i, head : head + 1, :], ref[i, head + 1 : head + 2, :]

    for copy in halo:
        copy.wait_recv()
    arrival(pq, part_s.at[0], part_r.at[0], partner).wait_recv()
    for c in range(chips):
        mine_c = part[core, c]
        num, best, total = merge([
            (mine_c[0:head], mine_c[head : head + 1], mine_c[head + 1 : head + 2]), read(pq, c)])
        pc[c, 0:head, :] = num
        pc[c, head:, :] = jnp.concatenate([best, total, jnp.zeros((6, cols), F32)], axis=0)
    for k in range(1, chips):
        there = lax.rem(chip + k, chips)
        part_send.append(send(pc.at[there], pr.at[k - 1], part_s.at[k], part_r.at[k], there * 2 + core))

    def window(b, carry):
        off = pl.multiple_of(b * QB, QB)
        q = qs[b]
        s = mm(q, kt[:, pl.ds(off, span)]) + tile[...] + kmask[:, pl.ds(off, span)]
        sg = mm(q, ktg[...])
        top = jnp.maximum(jnp.max(s, axis=1, keepdims=True), jnp.max(sg, axis=1, keepdims=True))
        e = jnp.exp(s - top)
        eg = jnp.exp(sg - top)
        total = jnp.sum(e, axis=1, keepdims=True) + jnp.sum(eg, axis=1, keepdims=True)
        o = mm(e.astype(BF16), vext[pl.ds(off, span), :]) + mm(eg.astype(BF16), vg[...])
        o = (o / total).astype(BF16)
        for h in range(heads):
            att[pl.ds(off, QB), h * head : (h + 1) * head] = o[h * QB : (h + 1) * QB]
        return carry

    lax.fori_loop(0, rows // QB, window, 0)

    loads[4].wait()

    def finish(b, carry):
        off = pl.multiple_of(b * 2 * QB, 2 * QB)
        o = mm(att[pl.ds(off, 2 * QB), :], wo_ref[...])
        h_ref[pl.ds(off, 2 * QB), :] = (x_ref[pl.ds(off, 2 * QB), :].astype(F32) + o).astype(BF16)
        return carry

    lax.fori_loop(0, rows // (2 * QB), finish, 0)

    for k in range(1, chips):
        arrival(pr.at[k - 1], part_s.at[k], part_r.at[k], partner).wait_recv()
    num, best, total = merge([read(pc, chip)] + [read(pr, k - 1) for k in range(1, chips)])
    og = (num / total).T.astype(BF16)
    ag = jnp.concatenate([og[h * share : (h + 1) * share] for h in range(heads)], axis=1)
    hg = xg[core * chips + chip].astype(F32) + mm(ag, wo_ref[...])
    h_ref[rows : rows + share, :] = hg.astype(BF16)
    for copy in halo + part_send:
        copy.wait_send()


def attention(sp, x, wq, wk, wv, wo, rel, gp, heads):
    rows, dim = x.shape
    head = wk.shape[1]
    width = (rel.shape[1] - 1) // 2
    span, ext = 2 * width + QB, rows + 2 * width
    n_glob = gp.shape[1]
    share, chips = n_glob // sp, sp // 2
    cols = heads * share
    anyspec = pl.BlockSpec(memory_space=pl.ANY)
    vmem = pl.BlockSpec(memory_space=pltpu.VMEM)
    dma = pltpu.SemaphoreType.DMA
    V = pltpu.VMEM
    return pl.pallas_call(
        functools.partial(attention_kernel, sp, heads),
        out_shape=jax.ShapeDtypeStruct((rows + share, dim), BF16),
        in_specs=[anyspec] * 5 + [vmem] * 2,
        out_specs=vmem,
        scratch_shapes=[
            V(x.shape, BF16), V(wq.shape, BF16), V(wk.shape, BF16), V(wv.shape, BF16), V(wo.shape, BF16),
            V((heads, span), F32), V((heads * QB, span), F32), V((ext, n_glob), BF16), V((1, ext), F32),
            V((head, ext), BF16), V((rows, head), BF16), V((head, rows), BF16), V((ext, head), BF16),
            V((rows // QB, heads * QB, head), BF16), V((sp, cols, head), BF16),
            V((head, n_glob), BF16), V((n_glob, head), BF16), V((rows, heads * head), BF16),
            V((2, chips, share, dim), BF16), V((chips, share, dim), BF16), V((chips, share, dim), BF16),
            V((chips - 1, share, dim), BF16), V((sp, share, dim), BF16),
            V((2, chips, head + 8, cols), F32), V((chips, head + 8, cols), F32),
            V((chips, head + 8, cols), F32), V((chips - 1, head + 8, cols), F32),
            dma((5,)), dma((4,)), dma((4,)), dma((chips,)), dma((chips,)), dma((chips,)), dma((chips,)),
            dma((chips,)), dma((chips,)),
        ],
        compiler_params=pltpu.CompilerParams(
            collective_id=0, has_side_effects=True, vmem_limit_bytes=VMEM_LIMIT),
        name='attend',
    )(x, wq, wk, wv, wo, rel, gp)


def ffn_kernel(sp, chunk, parts, h_ref, wu_hbm, wd_hbm, y_ref, yg_ref, wu, wd, acc, ubuf, gbuf, wu_sem, wd_sem, ssem, rsem):
    me = lax.axis_index('sp')
    chips = sp // 2
    chip, core = me // 2, lax.rem(me, 2)
    n_chunks = wu.shape[0]
    total = h_ref.shape[0]
    rows = y_ref.shape[0]
    share = total - rows
    tile = total // parts

    def up_copy(c):
        return pltpu.make_async_copy(wu_hbm.at[:, pl.ds(pl.multiple_of(c * chunk, chunk), chunk)], wu.at[c], wu_sem.at[c])

    def down_copy(c):
        return pltpu.make_async_copy(wd_hbm.at[pl.ds(pl.multiple_of(c * chunk, chunk), chunk), :], wd.at[c], wd_sem.at[c])

    def begin(c, carry):
        up_copy(c).start()
        down_copy(c).start()
        return carry

    lax.fori_loop(0, n_chunks, begin, 0)
    barrier = greet(sp)
    sends = []
    for p in range(parts):
        off = (parts - 1 - p) * tile
        hv = h_ref[off : off + tile, :]
        acc[...] = hv.astype(F32)

        def step(c, carry, p=p, off=off):
            if p == 0:
                up_copy(c).wait()
                down_copy(c).wait()
            z = mm(h_ref[off : off + tile, :], wu[c])
            u = jax.nn.gelu(z).astype(BF16)
            acc[...] += mm(u, wd[c])
            return carry

        lax.fori_loop(0, n_chunks, step, 0)
        y = acc[...].astype(BF16)
        if p == 0:
            y_ref[off:rows, :] = y[: tile - share]
            gbuf[core * chips + chip] = y[tile - share :]
            pl.semaphore_wait(barrier, sp - 1)
            sends = gather_blocks(gbuf, chips, chip, core, ssem, rsem)
        else:
            y_ref[off : off + tile, :] = y
        if p == 1:
            sends.append(gather_forward(gbuf, chips, chip, core, ssem, rsem))
    gather_finish(gbuf, chips, chip, core, ssem, rsem, sends)
    yg_ref[...] = gbuf[...].reshape(yg_ref.shape)


def ffn(sp, h, wu, wd, rows, chunk=384, parts=3):
    total, dim = h.shape
    hidden = wu.shape[1]
    share = total - rows
    n_chunks = hidden // chunk
    chips = sp // 2
    anyspec = pl.BlockSpec(memory_space=pl.ANY)
    vmem = pl.BlockSpec(memory_space=pltpu.VMEM)
    dma = pltpu.SemaphoreType.DMA
    V = pltpu.VMEM
    return pl.pallas_call(
        functools.partial(ffn_kernel, sp, chunk, parts),
        out_shape=(jax.ShapeDtypeStruct((rows, dim), BF16), jax.ShapeDtypeStruct((share * sp, dim), BF16)),
        in_specs=[vmem, anyspec, anyspec],
        out_specs=(vmem, vmem),
        scratch_shapes=[
            V((n_chunks, dim, chunk), BF16), V((n_chunks, chunk, dim), BF16), V((total // parts, dim), F32),
            V((total // parts, chunk), BF16), V((sp, share, dim), BF16),
            dma((n_chunks,)), dma((n_chunks,)), dma((chips,)), dma((chips,)),
        ],
        compiler_params=pltpu.CompilerParams(
            collective_id=1, has_side_effects=True, vmem_limit_bytes=VMEM_LIMIT),
        name='feed',
    )(h, wu, wd)


def solution(mesh):
    sp = mesh.shape['sp']

    def shard_layer(hidden_in, w_query, w_key, w_value, w_out, w_up, w_down, rel_bias, glob_pos):
        rows, dim = hidden_in.shape
        heads, head = w_query.shape[1], w_query.shape[2]
        h = attention(
            sp, hidden_in, w_query.reshape(dim, heads * head), w_key.reshape(dim, head), w_value.reshape(dim, head),
            w_out.reshape(heads * head, dim), rel_bias, glob_pos[None, :], heads)
        y, y_glob = ffn(sp, h, w_up, w_down, rows)
        pos = lax.axis_index('sp') * rows + jnp.arange(rows)
        hit = pos[:, None] == glob_pos[None, :]
        placed = jnp.dot(hit.astype(BF16), y_glob, preferred_element_type=F32).astype(BF16)
        y_out = jnp.where(jnp.any(hit, axis=1)[:, None], placed, y)
        return y_out, y_glob

    return jax.shard_map(
        shard_layer, mesh=mesh,
        in_specs=(P(('dp', 'sp'), None), P(), P(), P(), P(), P(), P(), P(), P('dp')),
        out_specs=(P(('dp', 'sp'), None), P('dp', None)),
        check_vma=False)
```

time: 341 us -> 137 us (0.40); the launches traced: 336 us -> 137 us
  Pallas kernels: 0 us -> 127 us
  matrix products: 115 us -> 4.13 us
  local copies, waits for them, and re-layouts: 90.8 us -> 4.46 us
  waiting for transfers between devices: 53.8 us -> 0 us
  blocking collectives: 28 us -> 0 us
  other arithmetic: 26.8 us -> 0.37 us
  between operations: 14.4 us -> 0.68 us
  starting transfers between devices: 7.26 us -> 0 us
    pallas_call x0 -> x2, Pallas kernels: none -> 127 us  [the longest x1 71.6 us: ffn(): pl.pallas_call(functools.partial(ffn_kernel, sp, chunk, parts), out_shape...]
    dot_general x16 -> x1, matrix products: 115 us -> 4.13 us  [shard_layer(): jnp.dot(hit.astype(BF16), y_glob, preferred_element_type=F32).astype(BF16)]
    psum x3 -> x0, waiting for transfers between devices: 53.7 us -> none  [the longest x1 53.7 us: shard_layer(): return (y_out, lax.psum(y_pick, 'sp'))]
    unnamed x43 -> x6, local copies, waits for them, and re-layouts: 40.4 us -> 4.46 us
    another operation x2 -> x0, local copies, waits for them, and re-layouts: 20.8 us -> none  [bias_tile(): tiled = jnp.tile(padded, (1, width))[:, :3 * width * width]]
    reduce_sum x3 -> x0, other arithmetic: 17.4 us -> none  [the longest x2 16.8 us: window_attention(): norm_sum = prob_win.sum(-1) + prob_glob.sum(-1)]
    psum x1 -> x0, blocking collectives: 15.3 us -> none  [shard_layer(): lax.psum((total * rescale, weighted * rescale[..., None]), 'sp')]
    pmax x1 -> x0, blocking collectives: 12.8 us -> none  [shard_layer(): best = lax.pmax(top, 'sp')]
  transfers between devices with their start and end apart: 5 -> 0, of which waited for: 1 -> 0; matrix products, arithmetic and copies ran while one was open for 49% -> 0% of each run, Pallas kernels for 0% -> 0%
where the time goes in v1:
time: 137 us
  Pallas kernels  127 us (93%)
  local copies, waits for them, and re-layouts  4.46 us (3%)
  matrix products  4.13 us (3%)
    pallas_call x1, Pallas kernels, ffn(): pl.pallas_call(functools.partial(ffn_kernel, sp, chunk, parts), out_shape...  71.6 us
    pallas_call x1, Pallas kernels, attention(): pl.pallas_call(functools.partial(attention_kernel, sp, heads), out_shape=...  55.5 us
    unnamed x6, local copies, waits for them, and re-layouts  4.46 us
    dot_general x1, matrix products, shard_layer(): jnp.dot(hit.astype(BF16), y_glob, preferred_element_type=F32).astype(BF16)  4.13 us

profile of v1, /device:TPU:81, one launch (start us, length us, event | category | flops | bytes accessed | tf_op | source)
XLA Modules:
  0.0 136.8 jit_solution(5952258946677699602)
XLA Ops:
  0.6 3.6 %copy.11 = bf16[144,8,4,256]{3,1,2,0:T(8,128)(2,1)} copy(bf16[144,8,4,256]{3,2,1,0:T(4,128)(2,1)} %bitcast.8) | data formatting | bytes 4718592
  4.3 55.5 %attend.1.h_ref = bf16[1056,1152]{1,0:T(8,128)(2,1)} custom-call(bf16[1024,1152]{1,0:T(8,128)(2,1)} %x_hbm.1, bf16[1152,1024]{1,0:T(8,128)(2,1)} %bitcast.7, bf16[1152,256]{1,0:T(8,128)(2,1)} %bitcast.10, bf16[1152,256]{1,0:T(8,128)(2,1)} %bitcast.11, bf16[1024,1152]{1,0:T(8,128)(2,1)} %bitcast.9, f32[4,1025]{1,0:T(4,128)} %rel_ref.1, s32[1,256]{1,0:T(1,128)} %bitcast.12), custom_call_target="tpu_custom_call" | custom-call | tf_op jit(solution)/shard_map/attend/pallas_call | solution.py:267
  59.8 0.0 copy-start.1
  59.8 71.6 %feed.1 = (bf16[1024,1152]{1,0:T(8,128)(2,1)}, bf16[256,1152]{1,0:T(8,128)(2,1)}) custom-call(bf16[1056,1152]{1,0:T(8,128)(2,1)} %attend.1.h_ref, bf16[1152,6912]{1,0:T(8,128)(2,1)} %wu_hbm.1, bf16[6912,1152]{1,0:T(8,128)(2,1)} %wd_hbm.1), custom_call_target="tpu_custom_call" | custom-call | tf_op jit(solution)/shard_map/feed/pallas_call | solution.py:354
  131.4 0.0 copy-done.1
  131.4 0.4 compare_reduce_fusion
  131.8 0.0 copy-start
  131.8 4.1 %fusion = bf16[1024,1152]{1,0:T(8,128)(2,1)} fusion(bf16[1024,1152]{1,0:T(8,128)(2,1)} %get-tuple-element.5, bf16[256,1152]{1,0:T(8,128)(2,1)} %get-tuple-element.9, pred[1024]{0:T(1024)(128)(4,1)S(1)} %compare_reduce_fusion, s32[256]{0:T(256)S(1)} %copy-done.1, s32[1024]{0:T(1024)S(1)} %iota_add_fusion), kind=kOutput, calls=%fused_computation.1 | convolution fusion | flops 606601216 | bytes 5314560 | tf_op jit(solution)/shard_map/dot_general | solution.py:382
  136.0 0.0 copy-done
  136.0 0.8 copy.13
  (1 shorter events, 0.0 us)
Async XLA Ops:
  59.8 71.6 %copy-start.1 = (s32[256]{0:T(256)S(1)}, s32[256]{0:T(256)}, u32[]{:S(2)}) copy-start(s32[256]{0:T(256)} %param.17) | copy-start | bytes 3076
  131.8 4.1 %copy-start = (bf16[256,1152]{1,0:T(8,128)(2,1)S(1)}, bf16[256,1152]{1,0:T(8,128)(2,1)}, u32[]{:S(2)}) copy-start(bf16[256,1152]{1,0:T(8,128)(2,1)} %get-tuple-element.9) | copy-start | bytes 1769476

commit v2 on v0

v2 whole, which is shorter than its diff:
```python
import functools

import jax
import jax.numpy as jnp
from jax import lax
from jax.experimental import pallas as pl
from jax.experimental.pallas import tpu as pltpu
from jax.sharding import PartitionSpec as P

MESH = pl.DeviceIdType.MESH
F32 = jnp.float32
BF16 = jnp.bfloat16
QB = 128
VMEM_LIMIT = 60 * 1024 * 1024


def mm(a, b):
    return jnp.dot(a, b, preferred_element_type=F32)


def mm_ta(a, b):
    return lax.dot_general(a, b, (((0,), (0,)), ((), ())), preferred_element_type=F32)


def mm_tb(a, b):
    return lax.dot_general(a, b, (((1,), (1,)), ((), ())), preferred_element_type=F32)


def send(src, dst, ssem, rsem, dev):
    copy = pltpu.make_async_remote_copy(
        src_ref=src, dst_ref=dst, send_sem=ssem, recv_sem=rsem, device_id={'sp': dev}, device_id_type=MESH)
    copy.start()
    return copy


def arrival(ref, ssem, rsem, dev):
    return pltpu.make_async_remote_copy(
        src_ref=ref, dst_ref=ref, send_sem=ssem, recv_sem=rsem, device_id={'sp': dev}, device_id_type=MESH)


def greet(sp):
    me = lax.axis_index('sp')
    barrier = pltpu.get_barrier_semaphore()
    for k in range(1, sp):
        pl.semaphore_signal(barrier, inc=1, device_id={'sp': lax.rem(me + k, sp)}, device_id_type=MESH)
    return barrier


class Place:
    def __init__(self, sp):
        me = lax.axis_index('sp')
        chips = sp // 2
        assert chips == 4
        self.me, self.chips = me, chips
        self.chip, self.core = me // 2, lax.rem(me, 2)
        self.nxt = lax.rem(self.chip + 1 - 2 * self.core + chips, chips)
        self.prv = lax.rem(self.chip - 1 + 2 * self.core + chips, chips)
        self.far = lax.rem(self.chip + 2, chips)
        self.to_nxt, self.to_prv = self.nxt * 2 + self.core, self.prv * 2 + self.core
        self.partner = self.chip * 2 + 1 - self.core
        self.base, self.other = self.core * chips, (1 - self.core) * chips


class Gather:
    def __init__(self, at, buf, ss, rs):
        self.at, self.buf, self.ss, self.rs = at, buf, ss, rs

    def push(self, chip, k, dev):
        ref = self.buf.at[self.at.base + chip]
        send(ref, ref, self.ss.at[k], self.rs.at[k], dev)

    def landed(self, slot, k):
        arrival(self.buf.at[slot], self.ss.at[k], self.rs.at[k], self.at.partner).wait_recv()

    def start(self):
        at = self.at
        self.push(at.chip, 0, at.to_nxt)
        self.push(at.chip, 1, at.to_prv)
        self.push(at.chip, 3, at.partner)

    def hop(self):
        at = self.at
        self.landed(at.base + at.prv, 0)
        self.push(at.prv, 2, at.to_nxt)
        self.push(at.prv, 4, at.partner)

    def end(self):
        at = self.at
        self.landed(at.base + at.nxt, 1)
        self.push(at.nxt, 5, at.partner)
        self.landed(at.base + at.far, 2)
        self.push(at.far, 6, at.partner)

    def finish(self):
        at = self.at
        for k, chip in ((3, at.chip), (4, at.nxt), (5, at.prv), (6, at.far)):
            self.landed(at.other + chip, k)
        for k, chip in ((0, at.chip), (1, at.chip), (2, at.prv), (3, at.chip), (4, at.prv), (5, at.nxt), (6, at.far)):
            arrival(self.buf.at[at.base + chip], self.ss.at[k], self.rs.at[k], at.partner).wait_send()


def merge(head, blocks):
    best = functools.reduce(jnp.maximum, [v[head : head + 1] for v in blocks])
    num, total = 0.0, 0.0
    for v in blocks:
        f = jnp.exp(v[head : head + 1] - best)
        num = num + v[0:head] * f
        total = total + v[head + 1 : head + 2] * f
    return num, best, total


def pack(ref, slot, head, num, best, total):
    ref[slot, 0:head, :] = num
    ref[slot, head:, :] = jnp.concatenate([best, total, jnp.zeros((6, best.shape[1]), F32)], axis=0)


def attention_kernel(sp, x_hbm, wq_hbm, wk_hbm, wv_hbm, wo_hbm, rel_ref, gp_ref, h_hbm, part_hbm, mine_hbm,
                     x_ref, wq3, wq_ref, wk_ref, wv_ref, wo_ref, rel_pad, tile, onehot, kmask,
                     kt, kloc, vt, vext, qs, qg, ktg, vg, num_ref, top_ref, sum_ref, att, h_ref,
                     xp, xq, xs, xr, xg, part, pq,
                     load_sem, out_sem, halo_s, halo_r, pick_s, pick_r, xg_s, xg_r, part_s, part_r):
    at = Place(sp)
    me, chips = at.me, at.chips
    rows, dim = x_ref.shape
    heads, head = wq3.shape[1:]
    width = (rel_ref.shape[1] - 1) // 2
    span = 2 * width + QB
    n_glob = gp_ref.shape[1]
    share = n_glob // sp
    cols = heads * share
    ext = rows + 2 * width
    seq = rows * sp
    start = me * rows
    blocks = rows // QB
    scale = head ** -0.5

    loads = []
    for i, (src, dst) in enumerate(((x_hbm, x_ref), (wk_hbm, wk_ref), (wv_hbm, wv_ref), (wq_hbm, wq3), (wo_hbm, wo_ref))):
        copy = pltpu.make_async_copy(src, dst, load_sem.at[i])
        copy.start()
        loads.append(copy)
    barrier = greet(sp)

    pos = start - width + lax.broadcasted_iota(jnp.int32, (ext, n_glob), 0)
    onehot[...] = jnp.where(pos == gp_ref[...], 1.0, 0.0).astype(BF16)

    loads[0].wait()
    picked = mm_ta(onehot[width : width + rows, :], x_ref[...]).astype(BF16)
    xp[...] = picked.reshape(xp.shape)
    pl.semaphore_wait(barrier, sp - 1)
    pick_send = [send(xp.at[1 - at.core], xq, pick_s.at[0], pick_r.at[0], at.partner)]

    loads[1].wait()
    k32 = mm(x_ref[...], wk_ref[...])
    kloc[...] = k32.astype(BF16)
    kt[:, width : width + rows] = k32.T.astype(BF16)

    arrival(xq, pick_s.at[0], pick_r.at[0], at.partner).wait_recv()
    xs[...] = xp[at.core] + xq[...]
    pick_send.append(send(xs.at[at.far], xr.at[2], pick_s.at[2], pick_r.at[2], at.to_nxt))
    pick_send.append(send(xs.at[at.prv], xr.at[1], pick_s.at[1], pick_r.at[1], at.to_prv))

    loads[2].wait()
    v32 = mm(x_ref[...], wv_ref[...])
    vext[width : width + rows, :] = v32.astype(BF16)
    vt[...] = v32.T.astype(BF16)
    right, left = lax.rem(me + 1, sp), lax.rem(me + sp - 1, sp)
    halo = [
        send(kt.at[:, pl.ds(rows, width)], kt.at[:, pl.ds(0, width)], halo_s.at[0], halo_r.at[0], right),
        send(kt.at[:, pl.ds(width, width)], kt.at[:, pl.ds(width + rows, width)], halo_s.at[1], halo_r.at[1], left),
        send(vext.at[pl.ds(rows, width)], vext.at[pl.ds(0, width)], halo_s.at[2], halo_r.at[2], right),
        send(vext.at[pl.ds(width, width)], vext.at[pl.ds(width + rows, width)], halo_s.at[3], halo_r.at[3], left),
    ]

    count = mm_tb(jnp.ones((8, n_glob), BF16), onehot[...])[0:1]
    col = start - width + lax.broadcasted_iota(jnp.int32, (1, ext), 1)
    kmask[...] = jnp.where((count > 0.5) | (col < 0) | (col >= seq), -jnp.inf, 0.0)
    rel_pad[...] = jnp.full(rel_pad.shape, -jnp.inf, F32)
    rel_pad[:, : 2 * width + 1] = rel_ref[...]
    for h in range(heads):
        line = jnp.broadcast_to(rel_pad[h : h + 1, :], (QB, span))
        tile[h * QB : (h + 1) * QB, :] = pltpu.roll(line, 0, 1, stride=1, stride_axis=0)

    loads[3].wait()
    wq_ref[...] = wq3[...].reshape(wq_ref.shape)

    arrival(xr.at[2], pick_s.at[2], pick_r.at[2], at.partner).wait_recv()
    xs[at.nxt] = xs[at.nxt] + xr[2]
    pick_send.append(send(xs.at[at.nxt], xr.at[0], pick_s.at[3], pick_r.at[3], at.to_nxt))

    for b in range(0, blocks, 2):
        qb = (mm(x_ref[b * QB : (b + 2) * QB, :], wq_ref[...]) * scale).astype(BF16)
        for r in range(2):
            for h in range(heads):
                qs[b + r, h * QB : (h + 1) * QB, :] = qb[r * QB : (r + 1) * QB, h * head : (h + 1) * head]

    arrival(xr.at[0], pick_s.at[3], pick_r.at[3], at.partner).wait_recv()
    arrival(xr.at[1], pick_s.at[1], pick_r.at[1], at.partner).wait_recv()
    xg[at.base + at.chip] = xs[at.chip] + xr[0] + xr[1]
    gather = Gather(at, xg, xg_s, xg_r)
    gather.start()
    outs = [pltpu.make_async_copy(xg.at[at.base + at.chip], mine_hbm, out_sem.at[0])]
    outs[0].start()

    def window(b):
        lo, hi = max(b * QB, width), min(b * QB + span, width + rows)
        s = mm(qs[b], kt[:, lo:hi]) + tile[:, lo - b * QB : hi - b * QB] + kmask[:, lo:hi]
        top = jnp.max(s, axis=1, keepdims=True)
        e = jnp.exp(s - top)
        total = jnp.sum(e, axis=1, keepdims=True)
        num_ref[b] = mm(e.astype(BF16), vext[lo:hi, :])
        top_ref[b] = jnp.broadcast_to(top, top_ref.shape[1:])
        sum_ref[b] = jnp.broadcast_to(total, sum_ref.shape[1:])

    for b in range(blocks // 2):
        window(b)
    gather.hop()
    for b in range(blocks // 2, blocks):
        window(b)
    gather.end()
    gather.finish()

    xgv = xg[...].reshape(n_glob, dim)
    ktg[...] = mm(xgv, wk_ref[...]).T.astype(BF16)
    vg[...] = mm(xgv, wv_ref[...]).astype(BF16)
    qgv = (mm(xgv, wq_ref[...]) * scale).astype(BF16)
    for r in range(sp):
        for h in range(heads):
            qg[r, h * share : (h + 1) * share, :] = qgv[r * share : (r + 1) * share, h * head : (h + 1) * head]

    for c in range(sp // 2):
        s = mm_tb(kloc[...], qg[2 * c : 2 * c + 2].reshape(2 * cols, head))
        top = jnp.max(s, axis=0, keepdims=True)
        e = jnp.exp(s - top)
        total = jnp.sum(e, axis=0, keepdims=True)
        num = mm(vt[...], e.astype(BF16))
        for r in range(2):
            here = slice(r * cols, (r + 1) * cols)
            pack(part, 2 * c + r, head, num[:, here], top[:, here], total[:, here])
    part_send = send(part.at[pl.ds(at.other, chips)], pq, part_s.at[0], part_r.at[0], at.partner)

    for copy in halo:
        copy.wait_recv()

    def complete(b):
        lo, hi = (b * QB, width) if b * QB < width else (width + rows, b * QB + span)
        s = mm(qs[b], kt[:, lo:hi]) + tile[:, lo - b * QB : hi - b * QB] + kmask[:, lo:hi]
        sg = mm(qs[b], ktg[...])
        top = top_ref[b]
        best = jnp.maximum(jnp.max(s, axis=1, keepdims=True), jnp.max(sg, axis=1, keepdims=True))
        best = jnp.maximum(top, best)
        fade = jnp.exp(top - best)
        e = [jnp.exp(s[:, i : i + QB] - best) for i in range(0, hi - lo, QB)]
        eg = [jnp.exp(sg[:, i : i + QB] - best) for i in range(0, n_glob, QB)]
        total = sum_ref[b] * fade + jnp.sum(functools.reduce(jnp.add, e + eg), axis=1, keepdims=True)
        o = mm(jnp.concatenate(e, axis=1).astype(BF16), vext[lo:hi, :])
        o = o + mm(jnp.concatenate(eg, axis=1).astype(BF16), vg[...])
        inv = 1.0 / total
        o = jnp.concatenate(
            [((num_ref[b, :, i : i + QB] * fade + o[:, i : i + QB]) * inv).astype(BF16) for i in range(0, head, QB)], axis=1)
        for h in range(heads):
            att[b * QB : (b + 1) * QB, h * head : (h + 1) * head] = o[h * QB : (h + 1) * QB]

    for b in range(blocks):
        complete(b)

    arrival(pq, part_s.at[0], part_r.at[0], at.partner).wait_recv()
    for c in range(chips):
        pack(pq, c, head, *merge(head, [part[at.base + c], pq[c]]))
    outs.append(pltpu.make_async_copy(pq, part_hbm, out_sem.at[1]))
    outs[-1].start()

    loads[4].wait()
    for b in range(0, blocks, 2):
        here = pl.ds(b * QB, 2 * QB)
        h_ref[here, :] = (x_ref[here, :].astype(F32) + mm(att[here, :], wo_ref[...])).astype(BF16)
        outs.append(pltpu.make_async_copy(h_ref.at[here], h_hbm.at[here], out_sem.at[2 + b // 2]))
        outs[-1].start()
    for copy in halo + pick_send + [part_send]:
        copy.wait_send()
    for copy in outs:
        copy.wait()


def attention(sp, x, wq, wk, wv, wo, rel, gp):
    rows, dim = x.shape
    heads, head = wq.shape[1:]
    width = (rel.shape[1] - 1) // 2
    span, ext = 2 * width + QB, rows + 2 * width
    n_glob = gp.shape[1]
    share, chips = n_glob // sp, sp // 2
    cols = heads * share
    blocks = rows // QB
    anyspec = pl.BlockSpec(memory_space=pl.ANY)
    vmem = pl.BlockSpec(memory_space=pltpu.VMEM)
    dma = pltpu.SemaphoreType.DMA
    V = pltpu.VMEM
    return pl.pallas_call(
        functools.partial(attention_kernel, sp),
        out_shape=(
            jax.ShapeDtypeStruct((rows, dim), BF16),
            jax.ShapeDtypeStruct((chips, head + 8, cols), F32),
            jax.ShapeDtypeStruct((share, dim), BF16)),
        in_specs=[anyspec] * 5 + [vmem] * 2,
        out_specs=(anyspec,) * 3,
        scratch_shapes=[
            V(x.shape, BF16), V(wq.shape, BF16), V((dim, heads * head), BF16), V(wk.shape, BF16), V(wv.shape, BF16), V(wo.shape, BF16),
            V((heads, span), F32), V((heads * QB, span), F32), V((ext, n_glob), BF16), V((1, ext), F32),
            V((head, ext), BF16), V((rows, head), BF16), V((head, rows), BF16), V((ext, head), BF16),
            V((blocks, heads * QB, head), BF16), V((sp, cols, head), BF16),
            V((head, n_glob), BF16), V((n_glob, head), BF16),
            V((blocks, heads * QB, head), F32), V((blocks, heads * QB, QB), F32), V((blocks, heads * QB, QB), F32),
            V((rows, heads * head), BF16), V((rows, dim), BF16),
            V((2, chips, share, dim), BF16), V((chips, share, dim), BF16), V((chips, share, dim), BF16),
            V((chips - 1, share, dim), BF16), V((sp, share, dim), BF16),
            V((sp, head + 8, cols), F32), V((chips, head + 8, cols), F32),
            dma((5,)), dma((2 + blocks // 2,)), dma((4,)), dma((4,)), dma((4,)), dma((4,)), dma((7,)), dma((7,)), dma((1,)), dma((1,)),
        ],
        compiler_params=pltpu.CompilerParams(
            collective_id=0, has_side_effects=True, vmem_limit_bytes=VMEM_LIMIT),
        name='attend',
    )(x, wq, wk, wv, wo, rel, gp)


def gelu(z):
    c = (2.0 / jnp.pi) ** 0.5
    hz = 0.5 * z
    return (hz + hz * jnp.tanh(z * (c + (c * 0.044715) * (z * z)))).astype(BF16)


def ffn_kernel(sp, chunk, group, small, h_hbm, part_hbm, mine_hbm, wo_hbm, wu_hbm, wd_hbm, y_hbm, yg_ref,
               hb, ybuf, wo_ref, wu, wd, acc, ubuf, gbuf, mine_ref, pc, pr,
               in_sem, out_sem, wu_sem, wd_sem, part_s, part_r, ssem, rsem):
    at = Place(sp)
    n_chunks = wu.shape[0]
    rows = ybuf.shape[0]
    share = mine_ref.shape[0]
    cols = pc.shape[2]
    head = pc.shape[1] - 8
    heads = cols // share
    first = rows + share - 2 * small
    cut = first + small - share

    def up(c):
        return pltpu.make_async_copy(wu_hbm.at[:, pl.ds(pl.multiple_of(c * chunk, chunk), chunk)], wu.at[c], wu_sem.at[c])

    def down(c):
        return pltpu.make_async_copy(wd_hbm.at[pl.ds(pl.multiple_of(c * chunk, chunk), chunk), :], wd.at[c], wd_sem.at[c])

    ins = [
        pltpu.make_async_copy(part_hbm, pc, in_sem.at[0]),
        pltpu.make_async_copy(h_hbm.at[pl.ds(0, first)], hb.at[pl.ds(0, first)], in_sem.at[1]),
        pltpu.make_async_copy(mine_hbm, mine_ref, in_sem.at[2]),
        pltpu.make_async_copy(h_hbm.at[pl.ds(first, cut - first)], hb.at[pl.ds(first, cut - first)], in_sem.at[3]),
        pltpu.make_async_copy(h_hbm.at[pl.ds(cut, rows - cut)], hb.at[pl.ds(cut + share, rows - cut)], in_sem.at[4]),
        pltpu.make_async_copy(wo_hbm, wo_ref, in_sem.at[5]),
    ]
    for copy in ins[:2]:
        copy.start()
    for c in range(n_chunks):
        up(c).start()
        down(c).start()
        if c == 2:
            for copy in ins[2:]:
                copy.start()
    barrier = greet(sp)

    def chunks(rows_of, c, n):
        m = rows_of.size
        for j in range(n):
            ubuf[j % 2, 0:m, :] = gelu(mm(hb[rows_of, :], wu[c + j]))
            if j:
                acc[0:m, :] += mm(ubuf[(j - 1) % 2, 0:m, :], wd[c + j - 1])
        acc[0:m, :] += mm(ubuf[(n - 1) % 2, 0:m, :], wd[c + n - 1])

    ins[0].wait()
    pl.semaphore_wait(barrier, sp - 1)
    send(pc.at[at.far], pr.at[2], part_s.at[2], part_r.at[2], at.to_nxt)
    send(pc.at[at.prv], pr.at[1], part_s.at[1], part_r.at[1], at.to_prv)

    ins[1].wait()
    tile0 = pl.ds(0, first)
    acc[0:first, :] = hb[tile0, :].astype(F32)

    def initial(g, carry):
        @pl.when(g == 1)
        def _():
            arrival(pr.at[2], part_s.at[2], part_r.at[2], at.partner).wait_recv()
            pack(pc, at.nxt, head, *merge(head, [pc[at.nxt], pr[2]]))
            send(pc.at[at.nxt], pr.at[0], part_s.at[0], part_r.at[0], at.to_nxt)

        for j in range(group):
            up(g * group + j).wait()
            down(g * group + j).wait()
        chunks(tile0, g * group, group)
        return carry

    lax.fori_loop(0, n_chunks // group, initial, 0)
    ybuf[tile0, :] = acc[0:first, :].astype(BF16)
    outs = [
        pltpu.make_async_copy(ybuf.at[tile0], y_hbm.at[tile0], out_sem.at[0]),
        pltpu.make_async_copy(ybuf.at[pl.ds(first, cut - first)], y_hbm.at[pl.ds(first, cut - first)], out_sem.at[1]),
        pltpu.make_async_copy(ybuf.at[pl.ds(cut, rows - cut)], y_hbm.at[pl.ds(cut, rows - cut)], out_sem.at[2]),
    ]
    outs[0].start()

    for copy in ins[2:]:
        copy.wait()
    for k in range(2):
        arrival(pr.at[k], part_s.at[k], part_r.at[k], at.partner).wait_recv()
    num, best, total = merge(head, [pc[at.chip], pr[0], pr[1]])
    og = (num / total).T.astype(BF16)
    ag = jnp.concatenate([og[h * share : (h + 1) * share] for h in range(heads)], axis=1)
    hb[cut : cut + share, :] = (mine_ref[...].astype(F32) + mm(ag, wo_ref[...])).astype(BF16)

    gather = Gather(at, gbuf, ssem, rsem)

    def later(p, carry):
        here = pl.ds(pl.multiple_of(first + p * small, share), small)
        acc[0:small, :] = hb[here, :].astype(F32)

        def some(g, carry):
            @pl.when((p == 1) & (g == 1))
            def _():
                gather.hop()

            @pl.when((p == 1) & (g == 2))
            def _():
                gather.end()

            chunks(here, g * group, group)
            return carry

        lax.fori_loop(0, n_chunks // group, some, 0)

        @pl.when(p == 0)
        def _():
            ybuf[first:cut, :] = acc[0 : small - share, :].astype(BF16)
            gbuf[at.base + at.chip] = acc[small - share : small, :].astype(BF16)
            gather.start()
            outs[1].start()

        return carry

    lax.fori_loop(0, 2, later, 0)
    ybuf[cut:rows, :] = acc[0:small, :].astype(BF16)
    outs[2].start()
    gather.finish()
    yg_ref[...] = gbuf[...].reshape(yg_ref.shape)
    for k, chip in ((0, at.nxt), (1, at.prv), (2, at.far)):
        arrival(pc.at[chip], part_s.at[k], part_r.at[k], at.partner).wait_send()
    for copy in outs:
        copy.wait()


def ffn(sp, h, part, mine, wo, wu, wd, chunk=768, group=3, small=320):
    rows, dim = h.shape
    share = mine.shape[0]
    n_chunks = wu.shape[1] // chunk
    assert n_chunks == 3 * group
    tile = rows + share - 2 * small
    anyspec = pl.BlockSpec(memory_space=pl.ANY)
    vmem = pl.BlockSpec(memory_space=pltpu.VMEM)
    dma = pltpu.SemaphoreType.DMA
    V = pltpu.VMEM
    return pl.pallas_call(
        functools.partial(ffn_kernel, sp, chunk, group, small),
        out_shape=(jax.ShapeDtypeStruct((rows, dim), BF16), jax.ShapeDtypeStruct((share * sp, dim), BF16)),
        in_specs=[anyspec] * 6,
        out_specs=(anyspec, vmem),
        scratch_shapes=[
            V((rows + share, dim), BF16), V((rows, dim), BF16), V(wo.shape, BF16),
            V((n_chunks, dim, chunk), BF16), V((n_chunks, chunk, dim), BF16), V((tile, dim), F32),
            V((2, tile, chunk), BF16), V((sp, share, dim), BF16),
            V((share, dim), BF16), V(part.shape, F32), V((3,) + part.shape[1:], F32),
            dma((6,)), dma((3,)), dma((n_chunks,)), dma((n_chunks,)), dma((3,)), dma((3,)), dma((7,)), dma((7,)),
        ],
        compiler_params=pltpu.CompilerParams(
            collective_id=1, has_side_effects=True, vmem_limit_bytes=VMEM_LIMIT),
        name='feed',
    )(h, part, mine, wo, wu, wd)


def place_kernel(y_ref, yg_ref, gp_ref, out_ref, outg_ref):
    n, n_glob = y_ref.shape[0], gp_ref.shape[1]
    first = lax.axis_index('sp') * n * pl.num_programs(0) + pl.program_id(0) * n
    pos = first + lax.broadcasted_iota(jnp.int32, (n, n_glob), 0)
    hit = jnp.where(pos == gp_ref[...], 1.0, 0.0)
    here = jnp.sum(hit, axis=1, keepdims=True) > 0.5
    out_ref[...] = jnp.where(here, mm(hit.astype(BF16), yg_ref[...]), y_ref[...].astype(F32)).astype(BF16)
    outg_ref[...] = yg_ref[...]


def place(y, y_glob, gp, steps=2):
    rows, dim = y.shape
    n = rows // steps
    whole = pl.BlockSpec(y_glob.shape, lambda i: (0, 0))
    return pl.pallas_call(
        place_kernel,
        grid=(steps,),
        out_shape=(jax.ShapeDtypeStruct(y.shape, BF16), jax.ShapeDtypeStruct(y_glob.shape, BF16)),
        in_specs=[pl.BlockSpec((n, dim), lambda i: (i, 0)), whole, pl.BlockSpec(gp.shape, lambda i: (0, 0))],
        out_specs=(pl.BlockSpec((n, dim), lambda i: (i, 0)), whole),
        name='place',
    )(y, y_glob, gp)


def solution(mesh):
    sp = mesh.shape['sp']

    def shard_layer(hidden_in, w_query, w_key, w_value, w_out, w_up, w_down, rel_bias, glob_pos):
        dim = hidden_in.shape[1]
        heads, head = w_query.shape[1], w_query.shape[2]
        gp = glob_pos[None, :]
        wo = w_out.reshape(heads * head, dim)
        h, part, mine = attention(
            sp, hidden_in, w_query, w_key.reshape(dim, head), w_value.reshape(dim, head), wo, rel_bias, gp)
        y, y_glob = ffn(sp, h, part, mine, wo, w_up, w_down)
        return place(y, y_glob, gp)

    return jax.shard_map(
        shard_layer, mesh=mesh,
        in_specs=(P(('dp', 'sp'), None), P(), P(), P(), P(), P(), P(), P(), P('dp')),
        out_specs=(P(('dp', 'sp'), None), P('dp', None)),
        check_vma=False)
```

time: 341 us -> 90.6 us (0.27); the launches traced: 336 us -> 90.5 us
  matrix products: 115 us -> 0 us
  local copies, waits for them, and re-layouts: 90.8 us -> 0 us
  Pallas kernels: 0 us -> 89.8 us
  waiting for transfers between devices: 53.8 us -> 0 us
  blocking collectives: 28 us -> 0 us
  other arithmetic: 26.8 us -> 0 us
  between operations: 14.4 us -> 0.65 us
  starting transfers between devices: 7.26 us -> 0 us
    dot_general x16 -> x0, matrix products: 115 us -> none  [the longest x1 26.8 us: finish_layer(): jnp.dot(hidden, w_up, preferred_element_type=jnp.float32)]
    pallas_call x0 -> x3, Pallas kernels: none -> 89.8 us  [the longest x1 50.3 us: ffn(): pl.pallas_call(functools.partial(ffn_kernel, sp, chunk, group, small), ou...]
    psum x3 -> x0, waiting for transfers between devices: 53.7 us -> none  [the longest x1 53.7 us: shard_layer(): return (y_out, lax.psum(y_pick, 'sp'))]
    unnamed x43 -> x0, local copies, waits for them, and re-layouts: 40.4 us -> none
    another operation x2 -> x0, local copies, waits for them, and re-layouts: 20.8 us -> none  [bias_tile(): tiled = jnp.tile(padded, (1, width))[:, :3 * width * width]]
    reduce_sum x3 -> x0, other arithmetic: 17.4 us -> none  [the longest x2 16.8 us: window_attention(): norm_sum = prob_win.sum(-1) + prob_glob.sum(-1)]
    psum x1 -> x0, blocking collectives: 15.3 us -> none  [shard_layer(): lax.psum((total * rescale, weighted * rescale[..., None]), 'sp')]
    pmax x1 -> x0, blocking collectives: 12.8 us -> none  [shard_layer(): best = lax.pmax(top, 'sp')]
  transfers between devices with their start and end apart: 5 -> 0, of which waited for: 1 -> 0; matrix products, arithmetic and copies ran while one was open for 49% -> 0% of each run, Pallas kernels for 0% -> 0%
where the time goes in v2:
time: 90.6 us; the launch traced here: 90.5 us
  Pallas kernels  89.8 us (99%)
    pallas_call x1, Pallas kernels, ffn(): pl.pallas_call(functools.partial(ffn_kernel, sp, chunk, group, small), ou...  50.3 us
    pallas_call x1, Pallas kernels, attention(): pl.pallas_call(functools.partial(attention_kernel, sp), out_shape=(jax.Sh...  35.9 us
    pallas_call x1, Pallas kernels, place(): pl.pallas_call(place_kernel, grid=(steps,), out_shape=(jax.ShapeDtypeStru...  3.68 us

profile of v2, /device:TPU:81, one launch (start us, length us, event | category | flops | bytes accessed | tf_op | source)
XLA Modules:
  0.0 90.5 jit_solution(6564557748938189193)
XLA Ops:
  0.6 35.9 %attend.1 = (bf16[1024,1152]{1,0:T(8,128)(2,1)}, f32[4,264,128]{2,1,0:T(8,128)}, bf16[32,1152]{1,0:T(8,128)(2,1)}) custom-call(bf16[1024,1152]{1,0:T(8,128)(2,1)} %x_hbm.1, bf16[1152,4,256]{2,1,0:T(4,128)(2,1)} %wq_hbm.1, bf16[1152,256]{1,0:T(8,128)(2,1)} %bitcast.6, bf16[1152,256]{1,0:T(8,128)(2,1)} %bitcast.7, bf16[1024,1152]{1,0:T(8,128)(2,1)} %bitcast.4, ...), custom_call_target="tpu_custom_call" | custom-call | tf_op jit(solution)/shard_map/attend/pallas_call | solution.py:298
  36.5 50.3 %feed.1 = (bf16[1024,1152]{1,0:T(8,128)(2,1)}, bf16[256,1152]{1,0:T(8,128)(2,1)}) custom-call(bf16[1024,1152]{1,0:T(8,128)(2,1)} %get-tuple-element.7.h_hbm, f32[4,264,128]{2,1,0:T(8,128)} %get-tuple-element.8.part_hbm, bf16[32,1152]{1,0:T(8,128)(2,1)} %get-tuple-element.9.mine_hbm, bf16[1024,1152]{1,0:T(8,128)(2,1)} %bitcast.5, bf16[1152,6912]{1,0:T(8,128)(2,1)} %wu_hbm.1, ...), custom_call_target="tpu_custom_call" | custom-call | tf_op jit(solution)/shard_map/feed/pallas_call | solution.py:466
  86.8 3.7 %place.1 = (bf16[1024,1152]{1,0:T(8,128)(2,1)}, bf16[256,1152]{1,0:T(8,128)(2,1)}) custom-call(bf16[1024,1152]{1,0:T(8,128)(2,1)} %get-tuple-element.10.y_ref, bf16[256,1152]{1,0:T(8,128)(2,1)} %get-tuple-element.11.yg_ref, s32[1,256]{1,0:T(1,128)} %bitcast.9), custom_call_target="tpu_custom_call" | custom-call | tf_op jit(solution)/shard_map/place/pallas_call | solution.py:498

commit v3 on v0

v3 whole, which is shorter than its diff:
```python
import functools

import jax
import jax.numpy as jnp
from jax import lax
from jax.experimental import pallas as pl
from jax.experimental.pallas import tpu as pltpu
from jax.sharding import PartitionSpec as P

MESH = pl.DeviceIdType.MESH
F32 = jnp.float32
BF16 = jnp.bfloat16
QB = 128
VMEM_LIMIT = 60 * 1024 * 1024


def mm(a, b):
    return jnp.dot(a, b, preferred_element_type=F32)


def mm_ta(a, b):
    return lax.dot_general(a, b, (((0,), (0,)), ((), ())), preferred_element_type=F32)


def mm_tb(a, b):
    return lax.dot_general(a, b, (((1,), (1,)), ((), ())), preferred_element_type=F32)


def send(src, dst, ssem, rsem, dev):
    copy = pltpu.make_async_remote_copy(
        src_ref=src, dst_ref=dst, send_sem=ssem, recv_sem=rsem, device_id={'sp': dev}, device_id_type=MESH)
    copy.start()
    return copy


def arrival(ref, ssem, rsem, dev):
    return pltpu.make_async_remote_copy(
        src_ref=ref, dst_ref=ref, send_sem=ssem, recv_sem=rsem, device_id={'sp': dev}, device_id_type=MESH)


def greet(sp):
    me = lax.axis_index('sp')
    barrier = pltpu.get_barrier_semaphore()
    for k in range(1, sp):
        pl.semaphore_signal(barrier, inc=1, device_id={'sp': lax.rem(me + k, sp)}, device_id_type=MESH)
    return barrier


class Place:
    def __init__(self, sp):
        me = lax.axis_index('sp')
        chips = sp // 2
        assert chips == 4
        self.me, self.chips = me, chips
        self.chip, self.core = me // 2, lax.rem(me, 2)
        self.nxt = lax.rem(self.chip + 1 - 2 * self.core + chips, chips)
        self.prv = lax.rem(self.chip - 1 + 2 * self.core + chips, chips)
        self.far = lax.rem(self.chip + 2, chips)
        self.to_nxt, self.to_prv = self.nxt * 2 + self.core, self.prv * 2 + self.core
        self.partner = self.chip * 2 + 1 - self.core
        self.base, self.other = self.core * chips, (1 - self.core) * chips


class Gather:
    def __init__(self, at, buf, ss, rs):
        self.at, self.buf, self.ss, self.rs = at, buf, ss, rs

    def push(self, chip, k, dev):
        ref = self.buf.at[self.at.base + chip]
        send(ref, ref, self.ss.at[k], self.rs.at[k], dev)

    def landed(self, slot, k):
        arrival(self.buf.at[slot], self.ss.at[k], self.rs.at[k], self.at.partner).wait_recv()

    def start(self):
        at = self.at
        self.push(at.chip, 0, at.to_nxt)
        self.push(at.chip, 1, at.to_prv)
        self.push(at.chip, 3, at.partner)

    def hop(self):
        at = self.at
        self.landed(at.base + at.prv, 0)
        self.push(at.prv, 2, at.to_nxt)
        self.push(at.prv, 4, at.partner)

    def end(self):
        at = self.at
        self.landed(at.base + at.nxt, 1)
        self.push(at.nxt, 5, at.partner)
        self.landed(at.base + at.far, 2)
        self.push(at.far, 6, at.partner)

    def finish(self):
        at = self.at
        for k, chip in ((3, at.chip), (4, at.nxt), (5, at.prv), (6, at.far)):
            self.landed(at.other + chip, k)
        for k, chip in ((0, at.chip), (1, at.chip), (2, at.prv), (3, at.chip), (4, at.prv), (5, at.nxt), (6, at.far)):
            arrival(self.buf.at[at.base + chip], self.ss.at[k], self.rs.at[k], at.partner).wait_send()


def merge(head, blocks):
    best = functools.reduce(jnp.maximum, [v[head : head + 1] for v in blocks])
    num, total = 0.0, 0.0
    for v in blocks:
        f = jnp.exp(v[head : head + 1] - best)
        num = num + v[0:head] * f
        total = total + v[head + 1 : head + 2] * f
    return num, best, total


def pack(ref, slot, head, num, best, total):
    ref[slot, 0:head, :] = num
    ref[slot, head:, :] = jnp.concatenate([best, total, jnp.zeros((6, best.shape[1]), F32)], axis=0)


def layer_kernel(sp, chunk, small, x_hbm, wq_hbm, wk_hbm, wv_hbm, wo_hbm, wu_hbm, wd_hbm, rel_ref, gp_ref, y_hbm, yg_ref,
                 x_ref, wo_ref, kt, vext, xp, xq, xs, xr, xg, part, pc, pr, hb, gbuf, wu_a, wd_a,
                 load_sem, out_sem, wu_sem, wd_sem, halo_s, halo_r, pick_s, pick_r, xg_s, xg_r, part_s, part_r, pass_s, pass_r, yg_s, yg_r):
    at = Place(sp)
    me, chips = at.me, at.chips
    rows, dim = x_ref.shape
    heads, head = wq_hbm.shape[1:]
    width = (rel_ref.shape[1] - 1) // 2
    span = 2 * width + QB
    n_glob = gp_ref.shape[1]
    share = n_glob // sp
    cols = heads * share
    ext = rows + 2 * width
    seq = rows * sp
    start = me * rows
    blocks = rows // QB
    scale = head ** -0.5
    n_chunks = wu_hbm.shape[1] // chunk
    early = wu_a.shape[0]
    first = rows + share - 2 * small
    cut = first + small - share

    def up_to(c, ref):
        return pltpu.make_async_copy(wu_hbm.at[:, pl.ds(pl.multiple_of(c * chunk, chunk), chunk)], ref, wu_sem.at[c])

    def down_to(c, ref):
        return pltpu.make_async_copy(wd_hbm.at[pl.ds(pl.multiple_of(c * chunk, chunk), chunk), :], ref, wd_sem.at[c])

    early_loads = [up_to(c, wu_a.at[c]) for c in range(early)] + [down_to(c, wd_a.at[c]) for c in range(early - 1)]
    right, left = lax.rem(me + 1, sp), lax.rem(me + sp - 1, sp)
    barrier = greet(sp)

    def attend(wq3, wq_ref, wk_ref, wv_ref, rel_pad, tile, onehot, kmask, kloc, vt, qs, qg, ktg, vg, num_ref, top_ref, sum_ref, att):
        loads = []
        for i, (src, dst) in enumerate(((x_hbm, x_ref), (wk_hbm, wk_ref), (wv_hbm, wv_ref), (wq_hbm, wq3), (wo_hbm, wo_ref))):
            loads.append(pltpu.make_async_copy(src, dst, load_sem.at[i]))
        loads[0].start()
        loads[1].start()

        pos = start - width + lax.broadcasted_iota(jnp.int32, (ext, n_glob), 0)
        onehot[...] = jnp.where(pos == gp_ref[...], 1.0, 0.0).astype(BF16)

        count = mm_tb(jnp.ones((8, n_glob), BF16), onehot[...])[0:1]
        col = start - width + lax.broadcasted_iota(jnp.int32, (1, ext), 1)
        kmask[...] = jnp.where((count > 0.5) | (col < 0) | (col >= seq), -jnp.inf, 0.0)
        rel_pad[...] = jnp.full(rel_pad.shape, -jnp.inf, F32)
        rel_pad[:, : 2 * width + 1] = rel_ref[...]
        for h in range(heads):
            line = jnp.broadcast_to(rel_pad[h : h + 1, :], (QB, span))
            tile[h * QB : (h + 1) * QB, :] = pltpu.roll(line, 0, 1, stride=1, stride_axis=0)

        def pick(rank):
            some = pl.ds(pl.multiple_of(rank * share, QB), chips * share)
            return mm_ta(onehot[width : width + rows, some], x_ref[...]).astype(BF16).reshape(xp.shape)

        loads[0].wait()
        for copy in loads[2:]:
            copy.start()
        xp[...] = pick(at.other)
        pl.semaphore_wait(barrier, sp - 1)
        pick_send = [send(xp, xq, pick_s.at[0], pick_r.at[0], at.partner)]
        xs[...] = pick(at.base)

        def key_rows(lo, hi):
            k32 = mm(x_ref[lo:hi, :], wk_ref[...])
            kloc[lo:hi, :] = k32.astype(BF16)
            kt[:, width + lo : width + hi] = k32.T.astype(BF16)

        loads[1].wait()
        key_rows(0, rows // 2)
        arrival(xq, pick_s.at[0], pick_r.at[0], at.partner).wait_recv()
        xs[...] = xs[...] + xq[...]
        pick_send.append(send(xs.at[at.far], xr.at[2], pick_s.at[2], pick_r.at[2], at.to_nxt))
        pick_send.append(send(xs.at[at.prv], xr.at[1], pick_s.at[1], pick_r.at[1], at.to_prv))
        key_rows(rows // 2, rows)

        loads[2].wait()
        v32 = mm(x_ref[...], wv_ref[...])
        vext[width : width + rows, :] = v32.astype(BF16)
        vt[...] = v32.T.astype(BF16)
        halo = [
            send(kt.at[:, pl.ds(rows, width)], kt.at[:, pl.ds(0, width)], halo_s.at[0], halo_r.at[0], right),
            send(kt.at[:, pl.ds(width, width)], kt.at[:, pl.ds(width + rows, width)], halo_s.at[1], halo_r.at[1], left),
            send(vext.at[pl.ds(rows, width)], vext.at[pl.ds(0, width)], halo_s.at[2], halo_r.at[2], right),
            send(vext.at[pl.ds(width, width)], vext.at[pl.ds(width + rows, width)], halo_s.at[3], halo_r.at[3], left),
        ]

        loads[3].wait()
        wq_ref[...] = wq3[...].reshape(wq_ref.shape)

        def project(b):
            qb = (mm(x_ref[b * QB : (b + 2) * QB, :], wq_ref[...]) * scale).astype(BF16)
            for r in range(2):
                for h in range(heads):
                    qs[b + r, h * QB : (h + 1) * QB, :] = qb[r * QB : (r + 1) * QB, h * head : (h + 1) * head]

        project(0)
        arrival(xr.at[2], pick_s.at[2], pick_r.at[2], at.partner).wait_recv()
        xs[at.nxt] = xs[at.nxt] + xr[2]
        pick_send.append(send(xs.at[at.nxt], xr.at[0], pick_s.at[3], pick_r.at[3], at.to_nxt))
        for b in range(2, blocks, 2):
            project(b)

        arrival(xr.at[0], pick_s.at[3], pick_r.at[3], at.partner).wait_recv()
        arrival(xr.at[1], pick_s.at[1], pick_r.at[1], at.partner).wait_recv()
        xg[at.base + at.chip] = xs[at.chip] + xr[0] + xr[1]
        gather = Gather(at, xg, xg_s, xg_r)
        gather.start()
        loads[4].wait()
        for copy in early_loads:
            copy.start()

        def window(b):
            lo = max(b * QB, width)
            hi = b * QB + span if b >= blocks // 2 else min(b * QB + span, width + rows)
            s = mm(qs[b], kt[:, lo:hi]) + tile[:, lo - b * QB : hi - b * QB] + kmask[:, lo:hi]
            top = jnp.max(s, axis=1, keepdims=True)
            e = jnp.exp(s - top)
            total = jnp.sum(e, axis=1, keepdims=True)
            num_ref[b] = mm(e.astype(BF16), vext[lo:hi, :])
            top_ref[b] = jnp.broadcast_to(top, top_ref.shape[1:])
            sum_ref[b] = jnp.broadcast_to(total, sum_ref.shape[1:])

        for b in range(blocks // 2):
            window(b)
        gather.hop()
        for copy in halo:
            copy.wait_recv()
        for b in range(blocks // 2, blocks):
            window(b)
        gather.end()

        def global_rows(rank):
            some = pl.ds(pl.multiple_of(rank * share, QB), chips * share)
            xgv = xg[pl.ds(rank, chips)].reshape(chips * share, dim)
            ktg[:, some] = mm(xgv, wk_ref[...]).T.astype(BF16)
            vg[some, :] = mm(xgv, wv_ref[...]).astype(BF16)
            qgv = (mm(xgv, wq_ref[...]) * scale).astype(BF16)
            for r in range(chips):
                for h in range(heads):
                    qg[r, h * share : (h + 1) * share, :] = qgv[r * share : (r + 1) * share, h * head : (h + 1) * head]
            for c in range(0, chips, 2):
                s = mm_tb(kloc[...], qg[c : c + 2].reshape(2 * cols, head))
                top = jnp.max(s, axis=0, keepdims=True)
                e = jnp.exp(s - top)
                total = jnp.sum(e, axis=0, keepdims=True)
                num = mm(vt[...], e.astype(BF16))
                for r in range(2):
                    here = slice(r * cols, (r + 1) * cols)
                    pack(part, rank + c + r, head, num[:, here], top[:, here], total[:, here])

        def parity(i, carry):
            @pl.when(i == 1)
            def _():
                gather.finish()

            global_rows(lax.rem(at.core + i, 2) * chips)
            return carry

        lax.fori_loop(0, 2, parity, 0)
        part_send = send(part.at[pl.ds(at.other, chips)], pc, part_s.at[0], part_r.at[0], at.partner)

        def complete(b):
            lo, hi = b * QB, max(b * QB, width)
            scores = [(mm(qs[b], ktg[...]), vg[...])]
            if lo < hi:
                s = mm(qs[b], kt[:, lo:hi]) + tile[:, : hi - lo] + kmask[:, lo:hi]
                scores.append((s, vext[lo:hi, :]))
            if b >= blocks // 2:
                scores = scores[:1]
            top = top_ref[b]
            best = top
            for s, _ in scores:
                best = jnp.maximum(best, jnp.max(s, axis=1, keepdims=True))
            fade = jnp.exp(top - best)
            o, sums = 0.0, 0.0
            for s, v in scores:
                e = [jnp.exp(s[:, i : i + QB] - best) for i in range(0, s.shape[1], QB)]
                sums = sums + functools.reduce(jnp.add, e)
                o = o + mm(jnp.concatenate(e, axis=1).astype(BF16), v)
            inv = 1.0 / (sum_ref[b] * fade + jnp.sum(sums, axis=1, keepdims=True))
            o = jnp.concatenate(
                [((num_ref[b, :, i : i + QB] * fade + o[:, i : i + QB]) * inv).astype(BF16) for i in range(0, head, QB)], axis=1)
            for h in range(heads):
                att[b * QB : (b + 1) * QB, h * head : (h + 1) * head] = o[h * QB : (h + 1) * QB]

        for b in range(blocks):
            complete(b)

        arrival(pc, part_s.at[0], part_r.at[0], at.partner).wait_recv()
        for c in range(chips):
            pack(pc, c, head, *merge(head, [part[at.base + c], pc[c]]))
        send(pc.at[at.far], pr.at[2], pass_s.at[2], pass_r.at[2], at.to_nxt)
        send(pc.at[at.prv], pr.at[1], pass_s.at[1], pass_r.at[1], at.to_prv)

        for b in range(0, blocks, 2):
            lo, hi = b * QB, (b + 2) * QB
            v = (x_ref[lo:hi, :].astype(F32) + mm(att[lo:hi, :], wo_ref[...])).astype(BF16)
            mid = min(max(cut, lo), hi)
            if lo < mid:
                hb[lo:mid, :] = v[: mid - lo]
            if mid < hi:
                hb[mid + share : hi + share, :] = v[mid - lo :]
        for copy in halo + pick_send + [part_send]:
            copy.wait_send()

    V = pltpu.VMEM
    pl.run_scoped(
        attend,
        V(wq_hbm.shape, BF16), V((dim, heads * head), BF16), V(wk_hbm.shape, BF16), V(wv_hbm.shape, BF16),
        V((heads, span), F32), V((heads * QB, span), F32), V((ext, n_glob), BF16), V((1, ext), F32),
        V((rows, head), BF16), V((head, rows), BF16), V((blocks, heads * QB, head), BF16), V((chips, cols, head), BF16),
        V((head, n_glob), BF16), V((n_glob, head), BF16),
        V((blocks, heads * QB, head), F32), V((blocks, heads * QB, QB), F32), V((blocks, heads * QB, QB), F32),
        V((rows, heads * head), BF16))

    def feed(wu_b, wd_b, ybuf, acc, ubuf):
        trips = (n_chunks - early) // 2

        def fetch(g):
            for j in range(2):
                up_to(early + 2 * g + j, wu_b.at[2 * g + j]).start()
                down_to(early + 2 * g + j - 1, wd_b.at[2 * g + j]).start()

        def fetched(g):
            for j in range(2):
                up_to(early + 2 * g + j, wu_b.at[2 * g + j]).wait()
                down_to(early + 2 * g + j - 1, wd_b.at[2 * g + j]).wait()

        last = down_to(n_chunks - 1, wd_b.at[2 * trips])
        fetch(0)

        arrival(pr.at[2], pass_s.at[2], pass_r.at[2], at.partner).wait_recv()
        pack(pc, at.nxt, head, *merge(head, [pc[at.nxt], pr[2]]))
        send(pc.at[at.nxt], pr.at[0], pass_s.at[0], pass_r.at[0], at.to_nxt)
        for copy in early_loads:
            copy.wait()

        def open_tile(rows_of):
            m = rows_of.size
            acc[0:m, :] = hb[rows_of, :].astype(F32)
            for c in range(early):
                ubuf[c % 2, 0:m, :] = gelu(mm(hb[rows_of, :], wu_a[c]))
                if c:
                    acc[0:m, :] += mm(ubuf[(c - 1) % 2, 0:m, :], wd_a[c - 1])

        def two_chunks(rows_of, g):
            m = rows_of.size
            for j in range(2):
                ubuf[1 - j, 0:m, :] = gelu(mm(hb[rows_of, :], wu_b[2 * g + j]))
                acc[0:m, :] += mm(ubuf[j, 0:m, :], wd_b[2 * g + j])

        def close_tile(rows_of):
            m = rows_of.size
            return (acc[0:m, :] + mm(ubuf[0, 0:m, :], wd_b[2 * trips])).astype(BF16)

        tile0 = pl.ds(0, first)
        open_tile(tile0)

        def initial(g, carry):
            fetched(g)

            @pl.when(g < trips - 1)
            def _():
                fetch(g + 1)

            @pl.when(g == trips - 1)
            def _():
                last.start()

            two_chunks(tile0, g)
            return carry

        lax.fori_loop(0, trips, initial, 0)
        last.wait()

        for k in range(2):
            arrival(pr.at[k], pass_s.at[k], pass_r.at[k], at.partner).wait_recv()
        num, best, total = merge(head, [pc[at.chip], pr[0], pr[1]])
        og = (num / total).T.astype(BF16)
        ag = jnp.concatenate([og[h * share : (h + 1) * share] for h in range(heads)], axis=1)
        ybuf[tile0, :] = close_tile(tile0)
        hb[cut : cut + share, :] = (xg[at.base + at.chip].astype(F32) + mm(ag, wo_ref[...])).astype(BF16)
        outs = [
            pltpu.make_async_copy(ybuf.at[tile0], y_hbm.at[tile0], out_sem.at[0]),
            pltpu.make_async_copy(ybuf.at[pl.ds(first, cut - first)], y_hbm.at[pl.ds(first, cut - first)], out_sem.at[1]),
            pltpu.make_async_copy(ybuf.at[pl.ds(cut, rows - cut)], y_hbm.at[pl.ds(cut, rows - cut)], out_sem.at[2]),
        ]
        outs[0].start()

        gather = Gather(at, gbuf, yg_s, yg_r)

        def later(p, carry):
            here = pl.ds(pl.multiple_of(first + p * small, share), small)
            open_tile(here)

            def some(g, carry):
                @pl.when((p == 1) & (g == 0))
                def _():
                    gather.hop()

                @pl.when((p == 1) & (g == trips - 1))
                def _():
                    gather.end()

                two_chunks(here, g)
                return carry

            lax.fori_loop(0, trips, some, 0)
            y = close_tile(here)

            @pl.when(p == 0)
            def _():
                ybuf[first:cut, :] = y[0 : small - share]
                gbuf[at.base + at.chip] = y[small - share :]
                gather.start()
                outs[1].start()

            @pl.when(p == 1)
            def _():
                ybuf[cut:rows, :] = y
                outs[2].start()

            return carry

        lax.fori_loop(0, 2, later, 0)
        gather.finish()
        yg_ref[...] = gbuf[...].reshape(yg_ref.shape)
        for k, chip in ((0, at.nxt), (1, at.prv), (2, at.far)):
            arrival(pc.at[chip], pass_s.at[k], pass_r.at[k], at.partner).wait_send()
        for copy in outs:
            copy.wait()

    late = n_chunks - early
    pl.run_scoped(
        feed,
        V((late, dim, chunk), BF16), V((late + 1, chunk, dim), BF16), V((rows, dim), BF16), V((first, dim), F32),
        V((2, first, chunk), BF16))


def layer(sp, x, wq, wk, wv, wo, wu, wd, rel, gp, chunk=768, small=320, early=3):
    rows, dim = x.shape
    heads, head = wq.shape[1:]
    width = (rel.shape[1] - 1) // 2
    ext = rows + 2 * width
    n_glob = gp.shape[1]
    share, chips = n_glob // sp, sp // 2
    cols = heads * share
    n_chunks = wu.shape[1] // chunk
    assert (n_chunks - early) % 2 == 0
    anyspec = pl.BlockSpec(memory_space=pl.ANY)
    vmem = pl.BlockSpec(memory_space=pltpu.VMEM)
    dma = pltpu.SemaphoreType.DMA
    V = pltpu.VMEM
    return pl.pallas_call(
        functools.partial(layer_kernel, sp, chunk, small),
        out_shape=(jax.ShapeDtypeStruct((rows, dim), BF16), jax.ShapeDtypeStruct((n_glob, dim), BF16)),
        in_specs=[anyspec] * 7 + [vmem] * 2,
        out_specs=(anyspec, vmem),
        scratch_shapes=[
            V(x.shape, BF16), V(wo.shape, BF16), V((head, ext), BF16), V((ext, head), BF16),
            V((chips, share, dim), BF16), V((chips, share, dim), BF16), V((chips, share, dim), BF16),
            V((chips - 1, share, dim), BF16), V((sp, share, dim), BF16),
            V((sp, head + 8, cols), F32), V((chips, head + 8, cols), F32), V((3, head + 8, cols), F32),
            V((rows + share, dim), BF16), V((sp, share, dim), BF16),
            V((early, dim, chunk), BF16), V((early - 1, chunk, dim), BF16),
            dma((5,)), dma((3,)), dma((n_chunks,)), dma((n_chunks,)),
            dma((4,)), dma((4,)), dma((4,)), dma((4,)), dma((7,)), dma((7,)), dma((1,)), dma((1,)), dma((3,)), dma((3,)),
            dma((7,)), dma((7,)),
        ],
        compiler_params=pltpu.CompilerParams(
            collective_id=0, has_side_effects=True, vmem_limit_bytes=VMEM_LIMIT),
        name='layer',
    )(x, wq, wk, wv, wo, wu, wd, rel, gp)


def gelu(z):
    c = (2.0 / jnp.pi) ** 0.5
    hz = 0.5 * z
    return (hz + hz * jnp.tanh(z * (c + (c * 0.044715) * (z * z)))).astype(BF16)


def place_kernel(y_ref, yg_ref, gp_ref, out_ref, outg_ref):
    n, n_glob = y_ref.shape[0], gp_ref.shape[1]
    first = lax.axis_index('sp') * n * pl.num_programs(0) + pl.program_id(0) * n
    pos = first + lax.broadcasted_iota(jnp.int32, (n, n_glob), 0)
    hit = jnp.where(pos == gp_ref[...], 1.0, 0.0)
    here = jnp.sum(hit, axis=1, keepdims=True) > 0.5
    out_ref[...] = jnp.where(here, mm(hit.astype(BF16), yg_ref[...]).astype(BF16), y_ref[...])
    outg_ref[...] = yg_ref[...]


def place(y, y_glob, gp, steps=2):
    rows, dim = y.shape
    n = rows // steps
    whole = pl.BlockSpec(y_glob.shape, lambda i: (0, 0))
    return pl.pallas_call(
        place_kernel,
        grid=(steps,),
        out_shape=(jax.ShapeDtypeStruct(y.shape, BF16), jax.ShapeDtypeStruct(y_glob.shape, BF16)),
        in_specs=[pl.BlockSpec((n, dim), lambda i: (i, 0)), whole, pl.BlockSpec(gp.shape, lambda i: (0, 0))],
        out_specs=(pl.BlockSpec((n, dim), lambda i: (i, 0)), whole),
        name='place',
    )(y, y_glob, gp)


def solution(mesh):
    sp = mesh.shape['sp']

    def shard_layer(hidden_in, w_query, w_key, w_value, w_out, w_up, w_down, rel_bias, glob_pos):
        dim = hidden_in.shape[1]
        heads, head = w_query.shape[1], w_query.shape[2]
        gp = glob_pos[None, :]
        wo = w_out.reshape(heads * head, dim)
        y, y_glob = layer(
            sp, hidden_in, w_query, w_key.reshape(dim, head), w_value.reshape(dim, head), wo, w_up, w_down, rel_bias, gp)
        return place(y, y_glob, gp)

    return jax.shard_map(
        shard_layer, mesh=mesh,
        in_specs=(P(('dp', 'sp'), None), P(), P(), P(), P(), P(), P(), P(), P('dp')),
        out_specs=(P(('dp', 'sp'), None), P('dp', None)),
        check_vma=False)
```

time: 341 us -> 85.4 us (0.25); the launches traced: 336 us -> 84.6 us
  matrix products: 115 us -> 0 us
  local copies, waits for them, and re-layouts: 90.8 us -> 0 us
  Pallas kernels: 0 us -> 84 us
  waiting for transfers between devices: 53.8 us -> 0 us
  blocking collectives: 28 us -> 0 us
  other arithmetic: 26.8 us -> 0 us
  between operations: 14.4 us -> 0.64 us
  starting transfers between devices: 7.26 us -> 0 us
    dot_general x16 -> x0, matrix products: 115 us -> none  [the longest x1 26.8 us: finish_layer(): jnp.dot(hidden, w_up, preferred_element_type=jnp.float32)]
    pallas_call x0 -> x2, Pallas kernels: none -> 84 us  [the longest x1 80.3 us: layer(): pl.pallas_call(functools.partial(layer_kernel, sp, chunk, small), out_sha...]
    psum x3 -> x0, waiting for transfers between devices: 53.7 us -> none  [the longest x1 53.7 us: shard_layer(): return (y_out, lax.psum(y_pick, 'sp'))]
    unnamed x43 -> x0, local copies, waits for them, and re-layouts: 40.4 us -> none
    another operation x2 -> x0, local copies, waits for them, and re-layouts: 20.8 us -> none  [bias_tile(): tiled = jnp.tile(padded, (1, width))[:, :3 * width * width]]
    reduce_sum x3 -> x0, other arithmetic: 17.4 us -> none  [the longest x2 16.8 us: window_attention(): norm_sum = prob_win.sum(-1) + prob_glob.sum(-1)]
    psum x1 -> x0, blocking collectives: 15.3 us -> none  [shard_layer(): lax.psum((total * rescale, weighted * rescale[..., None]), 'sp')]
    pmax x1 -> x0, blocking collectives: 12.8 us -> none  [shard_layer(): best = lax.pmax(top, 'sp')]
  transfers between devices with their start and end apart: 5 -> 0, of which waited for: 1 -> 0; matrix products, arithmetic and copies ran while one was open for 49% -> 0% of each run, Pallas kernels for 0% -> 0%
where the time goes in v3:
time: 85.4 us; the launch traced here: 84.6 us
  Pallas kernels  84 us (98%)
    pallas_call x1, Pallas kernels, layer(): pl.pallas_call(functools.partial(layer_kernel, sp, chunk, small), out_sha...  80.3 us
    pallas_call x1, Pallas kernels, place(): pl.pallas_call(place_kernel, grid=(steps,), out_shape=(jax.ShapeDtypeStru...  3.68 us

profile of v3, /device:TPU:81, one launch (start us, length us, event | category | flops | bytes accessed | tf_op | source)
XLA Modules:
  0.0 84.6 jit_solution(16887989199885112651)
XLA Ops:
  0.6 80.3 %layer.1 = (bf16[1024,1152]{1,0:T(8,128)(2,1)}, bf16[256,1152]{1,0:T(8,128)(2,1)}) custom-call(bf16[1024,1152]{1,0:T(8,128)(2,1)} %x_hbm.1, bf16[1152,4,256]{2,1,0:T(4,128)(2,1)} %wq_hbm.1, bf16[1152,256]{1,0:T(8,128)(2,1)} %bitcast.5, bf16[1152,256]{1,0:T(8,128)(2,1)} %bitcast.6, bf16[1024,1152]{1,0:T(8,128)(2,1)} %bitcast.4, bf16[1152,6912]{1,0:T(8,128)(2,1)} %wu_hbm.1, ...), custom_call_target="tpu_custom_call" | custom-call | tf_op jit(solution)/shard_map/layer/pallas_call | solution.py:471
  80.9 3.7 %place.1 = (bf16[1024,1152]{1,0:T(8,128)(2,1)}, bf16[256,1152]{1,0:T(8,128)(2,1)}) custom-call(bf16[1024,1152]{1,0:T(8,128)(2,1)} %get-tuple-element.4.y_ref, bf16[256,1152]{1,0:T(8,128)(2,1)} %get-tuple-element.5.yg_ref, s32[1,256]{1,0:T(1,128)} %bitcast.8), custom_call_target="tpu_custom_call" | custom-call | tf_op jit(solution)/shard_map/place/pallas_call | solution.py:513

commit v4 on v3

--- a/solution.py
+++ b/solution.py
@@ -57,6 +57,7 @@
         self.prv = lax.rem(self.chip - 1 + 2 * self.core + chips, chips)
         self.far = lax.rem(self.chip + 2, chips)
         self.to_nxt, self.to_prv = self.nxt * 2 + self.core, self.prv * 2 + self.core
+        self.to_far = self.far * 2 + self.core
         self.partner = self.chip * 2 + 1 - self.core
         self.base, self.other = self.core * chips, (1 - self.core) * chips
 
@@ -75,13 +76,13 @@
     def start(self):
         at = self.at
         self.push(at.chip, 0, at.to_nxt)
+        self.push(at.chip, 2, at.to_far)
         self.push(at.chip, 1, at.to_prv)
         self.push(at.chip, 3, at.partner)
 
     def hop(self):
         at = self.at
         self.landed(at.base + at.prv, 0)
-        self.push(at.prv, 2, at.to_nxt)
         self.push(at.prv, 4, at.partner)
 
     def end(self):
@@ -95,7 +96,7 @@
         at = self.at
         for k, chip in ((3, at.chip), (4, at.nxt), (5, at.prv), (6, at.far)):
             self.landed(at.other + chip, k)
-        for k, chip in ((0, at.chip), (1, at.chip), (2, at.prv), (3, at.chip), (4, at.prv), (5, at.nxt), (6, at.far)):
+        for k, chip in ((0, at.chip), (1, at.chip), (2, at.chip), (3, at.chip), (4, at.prv), (5, at.nxt), (6, at.far)):
             arrival(self.buf.at[at.base + chip], self.ss.at[k], self.rs.at[k], at.partner).wait_send()
 
 
@@ -114,7 +115,7 @@
     ref[slot, head:, :] = jnp.concatenate([best, total, jnp.zeros((6, best.shape[1]), F32)], axis=0)
 
 
-def layer_kernel(sp, chunk, small, x_hbm, wq_hbm, wk_hbm, wv_hbm, wo_hbm, wu_hbm, wd_hbm, rel_ref, gp_ref, y_hbm, yg_ref,
+def layer_kernel(sp, chunk, small, x_hbm, wq_hbm, wk_hbm, wv_hbm, wo_hbm, wu_hbm, wd_hbm, rel_ref, gp_ref, y_hbm, yg_hbm,
                  x_ref, wo_ref, kt, vext, xp, xq, xs, xr, xg, part, pc, pr, hb, gbuf, wu_a, wd_a,
                  load_sem, out_sem, wu_sem, wd_sem, halo_s, halo_r, pick_s, pick_r, xg_s, xg_r, part_s, part_r, pass_s, pass_r, yg_s, yg_r):
     at = Place(sp)
@@ -133,8 +134,7 @@
     scale = head ** -0.5
     n_chunks = wu_hbm.shape[1] // chunk
     early = wu_a.shape[0]
-    first = rows + share - 2 * small
-    cut = first + small - share
+    cut = 2 * small - share
 
     def up_to(c, ref):
         return pltpu.make_async_copy(wu_hbm.at[:, pl.ds(pl.multiple_of(c * chunk, chunk), chunk)], ref, wu_sem.at[c])
@@ -186,7 +186,8 @@
         key_rows(0, rows // 2)
         arrival(xq, pick_s.at[0], pick_r.at[0], at.partner).wait_recv()
         xs[...] = xs[...] + xq[...]
-        pick_send.append(send(xs.at[at.far], xr.at[2], pick_s.at[2], pick_r.at[2], at.to_nxt))
+        pick_send.append(send(xs.at[at.far], xr.at[2], pick_s.at[2], pick_r.at[2], at.to_far))
+        pick_send.append(send(xs.at[at.nxt], xr.at[0], pick_s.at[3], pick_r.at[3], at.to_nxt))
         pick_send.append(send(xs.at[at.prv], xr.at[1], pick_s.at[1], pick_r.at[1], at.to_prv))
         key_rows(rows // 2, rows)
 
@@ -211,15 +212,13 @@
                     qs[b + r, h * QB : (h + 1) * QB, :] = qb[r * QB : (r + 1) * QB, h * head : (h + 1) * head]
 
         project(0)
-        arrival(xr.at[2], pick_s.at[2], pick_r.at[2], at.partner).wait_recv()
-        xs[at.nxt] = xs[at.nxt] + xr[2]
-        pick_send.append(send(xs.at[at.nxt], xr.at[0], pick_s.at[3], pick_r.at[3], at.to_nxt))
         for b in range(2, blocks, 2):
             project(b)
 
         arrival(xr.at[0], pick_s.at[3], pick_r.at[3], at.partner).wait_recv()
         arrival(xr.at[1], pick_s.at[1], pick_r.at[1], at.partner).wait_recv()
-        xg[at.base + at.chip] = xs[at.chip] + xr[0] + xr[1]
+        arrival(xr.at[2], pick_s.at[2], pick_r.at[2], at.partner).wait_recv()
+        xg[at.base + at.chip] = (xs[at.chip] + xr[0]) + (xr[1] + xr[2])
         gather = Gather(at, xg, xg_s, xg_r)
         gather.start()
         loads[4].wait()
@@ -331,20 +330,11 @@
         V((rows, heads * head), BF16))
 
     def feed(wu_b, wd_b, ybuf, acc, ubuf):
-        trips = (n_chunks - early) // 2
-
-        def fetch(g):
-            for j in range(2):
-                up_to(early + 2 * g + j, wu_b.at[2 * g + j]).start()
-                down_to(early + 2 * g + j - 1, wd_b.at[2 * g + j]).start()
-
-        def fetched(g):
-            for j in range(2):
-                up_to(early + 2 * g + j, wu_b.at[2 * g + j]).wait()
-                down_to(early + 2 * g + j - 1, wd_b.at[2 * g + j]).wait()
-
-        last = down_to(n_chunks - 1, wd_b.at[2 * trips])
-        fetch(0)
+        late_loads = [down_to(early - 1, wd_b.at[0])]
+        for c in range(early, n_chunks):
+            late_loads += [up_to(c, wu_b.at[c - early]), down_to(c, wd_b.at[c - early + 1])]
+        for copy in late_loads:
+            copy.start()
 
         arrival(pr.at[2], pass_s.at[2], pass_r.at[2], at.partner).wait_recv()
         pack(pc, at.nxt, head, *merge(head, [pc[at.nxt], pr[2]]))
@@ -352,96 +342,64 @@
         for copy in early_loads:
             copy.wait()
 
-        def open_tile(rows_of):
-            m = rows_of.size
-            acc[0:m, :] = hb[rows_of, :].astype(F32)
+        gather = Gather(at, gbuf, yg_s, yg_r)
+        ends = (0, small, 2 * small - share, rows)
+        outs = [
+            pltpu.make_async_copy(ybuf.at[pl.ds(a, b - a)], y_hbm.at[pl.ds(a, b - a)], out_sem.at[p])
+            for p, (a, b) in enumerate(zip(ends[:-1], ends[1:]))]
+
+        def one_tile(p, carry):
+            here = pl.ds(pl.multiple_of(p * small, share), small)
+            acc[...] = hb[here, :].astype(F32)
             for c in range(early):
-                ubuf[c % 2, 0:m, :] = gelu(mm(hb[rows_of, :], wu_a[c]))
+                ubuf[c % 2] = gelu(mm(hb[here, :], wu_a[c]))
                 if c:
-                    acc[0:m, :] += mm(ubuf[(c - 1) % 2, 0:m, :], wd_a[c - 1])
-
-        def two_chunks(rows_of, g):
-            m = rows_of.size
-            for j in range(2):
-                ubuf[1 - j, 0:m, :] = gelu(mm(hb[rows_of, :], wu_b[2 * g + j]))
-                acc[0:m, :] += mm(ubuf[j, 0:m, :], wd_b[2 * g + j])
-
-        def close_tile(rows_of):
-            m = rows_of.size
-            return (acc[0:m, :] + mm(ubuf[0, 0:m, :], wd_b[2 * trips])).astype(BF16)
-
-        tile0 = pl.ds(0, first)
-        open_tile(tile0)
-
-        def initial(g, carry):
-            fetched(g)
-
-            @pl.when(g < trips - 1)
-            def _():
-                fetch(g + 1)
-
-            @pl.when(g == trips - 1)
-            def _():
-                last.start()
-
-            two_chunks(tile0, g)
-            return carry
-
-        lax.fori_loop(0, trips, initial, 0)
-        last.wait()
-
-        for k in range(2):
-            arrival(pr.at[k], pass_s.at[k], pass_r.at[k], at.partner).wait_recv()
-        num, best, total = merge(head, [pc[at.chip], pr[0], pr[1]])
-        og = (num / total).T.astype(BF16)
-        ag = jnp.concatenate([og[h * share : (h + 1) * share] for h in range(heads)], axis=1)
-        ybuf[tile0, :] = close_tile(tile0)
-        hb[cut : cut + share, :] = (xg[at.base + at.chip].astype(F32) + mm(ag, wo_ref[...])).astype(BF16)
-        outs = [
-            pltpu.make_async_copy(ybuf.at[tile0], y_hbm.at[tile0], out_sem.at[0]),
-            pltpu.make_async_copy(ybuf.at[pl.ds(first, cut - first)], y_hbm.at[pl.ds(first, cut - first)], out_sem.at[1]),
-            pltpu.make_async_copy(ybuf.at[pl.ds(cut, rows - cut)], y_hbm.at[pl.ds(cut, rows - cut)], out_sem.at[2]),
-        ]
-        outs[0].start()
-
-        gather = Gather(at, gbuf, yg_s, yg_r)
-
-        def later(p, carry):
-            here = pl.ds(pl.multiple_of(first + p * small, share), small)
-            open_tile(here)
-
-            def some(g, carry):
-                @pl.when((p == 1) & (g == 0))
-                def _():
-                    gather.hop()
-
-                @pl.when((p == 1) & (g == trips - 1))
-                def _():
-                    gather.end()
-
-                two_chunks(here, g)
-                return carry
-
-            lax.fori_loop(0, trips, some, 0)
-            y = close_tile(here)
+                    acc[...] += mm(ubuf[(c - 1) % 2], wd_a[c - 1])
 
             @pl.when(p == 0)
             def _():
-                ybuf[first:cut, :] = y[0 : small - share]
+                for copy in late_loads:
+                    copy.wait()
+                for k in range(2):
+                    arrival(pr.at[k], pass_s.at[k], pass_r.at[k], at.partner).wait_recv()
+                num, best, total = merge(head, [pc[at.chip], pr[0], pr[1]])
+                og = (num / total).T.astype(BF16)
+                ag = jnp.concatenate([og[h * share : (h + 1) * share] for h in range(heads)], axis=1)
+                hb[cut : cut + share, :] = (xg[at.base + at.chip].astype(F32) + mm(ag, wo_ref[...])).astype(BF16)
+
+            @pl.when(p == 2)
+            def _():
+                gather.hop()
+                gather.end()
+
+            for c in range(early, n_chunks):
+                ubuf[c % 2] = gelu(mm(hb[here, :], wu_b[c - early]))
+                acc[...] += mm(ubuf[(c - 1) % 2], wd_b[c - early])
+            y = (acc[...] + mm(ubuf[(n_chunks - 1) % 2], wd_b[n_chunks - early])).astype(BF16)
+
+            @pl.when(p == 0)
+            def _():
+                ybuf[0:small, :] = y
+                outs[0].start()
+
+            @pl.when(p == 1)
+            def _():
+                ybuf[small:cut, :] = y[0 : small - share]
                 gbuf[at.base + at.chip] = y[small - share :]
                 gather.start()
                 outs[1].start()
 
-            @pl.when(p == 1)
+            @pl.when(p == 2)
             def _():
                 ybuf[cut:rows, :] = y
                 outs[2].start()
 
             return carry
 
-        lax.fori_loop(0, 2, later, 0)
+        lax.fori_loop(0, 3, one_tile, 0)
         gather.finish()
-        yg_ref[...] = gbuf[...].reshape(yg_ref.shape)
+        outs.append(pltpu.make_async_copy(gbuf, yg_hbm, out_sem.at[3]))
+        outs[3].start()
         for k, chip in ((0, at.nxt), (1, at.prv), (2, at.far)):
             arrival(pc.at[chip], pass_s.at[k], pass_r.at[k], at.partner).wait_send()
         for copy in outs:
@@ -450,11 +408,11 @@
     late = n_chunks - early
     pl.run_scoped(
         feed,
-        V((late, dim, chunk), BF16), V((late + 1, chunk, dim), BF16), V((rows, dim), BF16), V((first, dim), F32),
-        V((2, first, chunk), BF16))
-
-
-def layer(sp, x, wq, wk, wv, wo, wu, wd, rel, gp, chunk=768, small=320, early=3):
+        V((late, dim, chunk), BF16), V((late + 1, chunk, dim), BF16), V((rows, dim), BF16), V((small, dim), F32),
+        V((2, small, chunk), BF16))
+
+
+def layer(sp, x, wq, wk, wv, wo, wu, wd, rel, gp, chunk=768, early=5):
     rows, dim = x.shape
     heads, head = wq.shape[1:]
     width = (rel.shape[1] - 1) // 2
@@ -463,16 +421,16 @@
     share, chips = n_glob // sp, sp // 2
     cols = heads * share
     n_chunks = wu.shape[1] // chunk
-    assert (n_chunks - early) % 2 == 0
+    small = (rows + share) // 3
     anyspec = pl.BlockSpec(memory_space=pl.ANY)
     vmem = pl.BlockSpec(memory_space=pltpu.VMEM)
     dma = pltpu.SemaphoreType.DMA
     V = pltpu.VMEM
     return pl.pallas_call(
         functools.partial(layer_kernel, sp, chunk, small),
-        out_shape=(jax.ShapeDtypeStruct((rows, dim), BF16), jax.ShapeDtypeStruct((n_glob, dim), BF16)),
+        out_shape=(jax.ShapeDtypeStruct((rows, dim), BF16), jax.ShapeDtypeStruct((sp, share, dim), BF16)),
         in_specs=[anyspec] * 7 + [vmem] * 2,
-        out_specs=(anyspec, vmem),
+        out_specs=(anyspec, anyspec),
         scratch_shapes=[
             V(x.shape, BF16), V(wo.shape, BF16), V((head, ext), BF16), V((ext, head), BF16),
             V((chips, share, dim), BF16), V((chips, share, dim), BF16), V((chips, share, dim), BF16),
@@ -480,7 +438,7 @@
             V((sp, head + 8, cols), F32), V((chips, head + 8, cols), F32), V((3, head + 8, cols), F32),
             V((rows + share, dim), BF16), V((sp, share, dim), BF16),
             V((early, dim, chunk), BF16), V((early - 1, chunk, dim), BF16),
-            dma((5,)), dma((3,)), dma((n_chunks,)), dma((n_chunks,)),
+            dma((5,)), dma((4,)), dma((n_chunks,)), dma((n_chunks,)),
             dma((4,)), dma((4,)), dma((4,)), dma((4,)), dma((7,)), dma((7,)), dma((1,)), dma((1,)), dma((3,)), dma((3,)),
             dma((7,)), dma((7,)),
         ],
@@ -530,7 +488,7 @@
         wo = w_out.reshape(heads * head, dim)
         y, y_glob = layer(
             sp, hidden_in, w_query, w_key.reshape(dim, head), w_value.reshape(dim, head), wo, w_up, w_down, rel_bias, gp)
-        return place(y, y_glob, gp)
+        return place(y, y_glob.reshape(-1, dim), gp)
 
     return jax.shard_map(
         shard_layer, mesh=mesh,

time: 85.4 us -> 84.1 us (0.985)
  Pallas kernels: 84 us -> 82.9 us
    pallas_call x1, Pallas kernels: 80.3 us -> 79.2 us  [layer(): pl.pallas_call(functools.partial(layer_kernel, sp, chunk, small), out_sha...]
where the time goes in v4:
time: 84.1 us; the launch traced here: 83.5 us
  Pallas kernels  82.9 us (99%)
    pallas_call x1, Pallas kernels, layer(): pl.pallas_call(functools.partial(layer_kernel, sp, chunk, small), out_sha...  79.2 us
    pallas_call x1, Pallas kernels, place(): pl.pallas_call(place_kernel, grid=(steps,), out_shape=(jax.ShapeDtypeStru...  3.68 us

profile of v4, /device:TPU:81, one launch (start us, length us, event | category | flops | bytes accessed | tf_op | source)
XLA Modules:
  0.0 83.5 jit_solution(14717637526556441790)
XLA Ops:
  0.6 79.2 %layer.1 = (bf16[1024,1152]{1,0:T(8,128)(2,1)}, bf16[8,32,1152]{2,1,0:T(8,128)(2,1)}) custom-call(bf16[1024,1152]{1,0:T(8,128)(2,1)} %x_hbm.1, bf16[1152,4,256]{2,1,0:T(4,128)(2,1)} %wq_hbm.1, bf16[1152,256]{1,0:T(8,128)(2,1)} %bitcast.7, bf16[1152,256]{1,0:T(8,128)(2,1)} %bitcast.8, bf16[1024,1152]{1,0:T(8,128)(2,1)} %bitcast.5, bf16[1152,6912]{1,0:T(8,128)(2,1)} %wu_hbm.1, ...), custom_call_target="tpu_custom_call" | custom-call | tf_op jit(solution)/shard_map/layer/pallas_call | solution.py:429
  79.8 3.7 %place.1 = (bf16[1024,1152]{1,0:T(8,128)(2,1)}, bf16[256,1152]{1,0:T(8,128)(2,1)}) custom-call(bf16[1024,1152]{1,0:T(8,128)(2,1)} %get-tuple-element.4.y_ref, bf16[256,1152]{1,0:T(8,128)(2,1)} %bitcast.6, s32[1,256]{1,0:T(1,128)} %bitcast.10), custom_call_target="tpu_custom_call" | custom-call | tf_op jit(solution)/shard_map/place/pallas_call | solution.py:471

commit v5 on v4

--- a/solution.py
+++ b/solution.py
@@ -186,8 +186,7 @@
         key_rows(0, rows // 2)
         arrival(xq, pick_s.at[0], pick_r.at[0], at.partner).wait_recv()
         xs[...] = xs[...] + xq[...]
-        pick_send.append(send(xs.at[at.far], xr.at[2], pick_s.at[2], pick_r.at[2], at.to_far))
-        pick_send.append(send(xs.at[at.nxt], xr.at[0], pick_s.at[3], pick_r.at[3], at.to_nxt))
+        pick_send.append(send(xs.at[at.far], xr.at[2], pick_s.at[2], pick_r.at[2], at.to_nxt))
         pick_send.append(send(xs.at[at.prv], xr.at[1], pick_s.at[1], pick_r.at[1], at.to_prv))
         key_rows(rows // 2, rows)
 
@@ -212,13 +211,15 @@
                     qs[b + r, h * QB : (h + 1) * QB, :] = qb[r * QB : (r + 1) * QB, h * head : (h + 1) * head]
 
         project(0)
+        arrival(xr.at[2], pick_s.at[2], pick_r.at[2], at.partner).wait_recv()
+        xs[at.nxt] = xs[at.nxt] + xr[2]
+        pick_send.append(send(xs.at[at.nxt], xr.at[0], pick_s.at[3], pick_r.at[3], at.to_nxt))
         for b in range(2, blocks, 2):
             project(b)
 
         arrival(xr.at[0], pick_s.at[3], pick_r.at[3], at.partner).wait_recv()
         arrival(xr.at[1], pick_s.at[1], pick_r.at[1], at.partner).wait_recv()
-        arrival(xr.at[2], pick_s.at[2], pick_r.at[2], at.partner).wait_recv()
-        xg[at.base + at.chip] = (xs[at.chip] + xr[0]) + (xr[1] + xr[2])
+        xg[at.base + at.chip] = xs[at.chip] + xr[0] + xr[1]
         gather = Gather(at, xg, xg_s, xg_r)
         gather.start()
         loads[4].wait()

time: 84.1 us -> 83.9 us (level)
  no operation moved by 1% of the time
where the time goes in v5:
time: 83.9 us; the launch traced here: 83.3 us
  Pallas kernels  82.7 us (99%)
    pallas_call x1, Pallas kernels, layer(): pl.pallas_call(functools.partial(layer_kernel, sp, chunk, small), out_sha...  79 us
    pallas_call x1, Pallas kernels, place(): pl.pallas_call(place_kernel, grid=(steps,), out_shape=(jax.ShapeDtypeStru...  3.68 us

profile of v5, /device:TPU:81, one launch (start us, length us, event | category | flops | bytes accessed | tf_op | source)
XLA Modules:
  0.0 83.3 jit_solution(14190494190740900556)
XLA Ops:
  0.6 79.0 %layer.1 = (bf16[1024,1152]{1,0:T(8,128)(2,1)}, bf16[8,32,1152]{2,1,0:T(8,128)(2,1)}) custom-call(bf16[1024,1152]{1,0:T(8,128)(2,1)} %x_hbm.1, bf16[1152,4,256]{2,1,0:T(4,128)(2,1)} %wq_hbm.1, bf16[1152,256]{1,0:T(8,128)(2,1)} %bitcast.7, bf16[1152,256]{1,0:T(8,128)(2,1)} %bitcast.8, bf16[1024,1152]{1,0:T(8,128)(2,1)} %bitcast.5, bf16[1152,6912]{1,0:T(8,128)(2,1)} %wu_hbm.1, ...), custom_call_target="tpu_custom_call" | custom-call | tf_op jit(solution)/shard_map/layer/pallas_call | solution.py:430
  79.6 3.7 %place.1 = (bf16[1024,1152]{1,0:T(8,128)(2,1)}, bf16[256,1152]{1,0:T(8,128)(2,1)}) custom-call(bf16[1024,1152]{1,0:T(8,128)(2,1)} %get-tuple-element.4.y_ref, bf16[256,1152]{1,0:T(8,128)(2,1)} %bitcast.6, s32[1,256]{1,0:T(1,128)} %bitcast.10), custom_call_target="tpu_custom_call" | custom-call | tf_op jit(solution)/shard_map/place/pallas_call | solution.py:472
